TPU v7x, 16 devices: a whole 2x2x2 slice. The times are simulated.
16 devices in a mesh: fsdp: 16 (over z, y, x, core).
Axes of the slice: x: 2, y: 2, z: 2, core: 2. Of those that a mesh axis runs over, the one named last changes fastest.
Arguments:
- x_in: bfloat16 [16, 384, 1024], P('fsdp')
- positions: int32 [384], replicated
- grad_out: bfloat16 [16, 384, 1024], P('fsdp')
- ln_gamma_1: float32 [1024], P('fsdp')
- w_q_1: bfloat16 [1024, 2048], P('fsdp')
- w_k_1: bfloat16 [1024, 1024], P('fsdp')
- w_v_1: bfloat16 [1024, 1024], P('fsdp')
- w_o_1: bfloat16 [2048, 1024], P('fsdp')
- w_gate_1: bfloat16 [1024, 3072], P('fsdp')
- w_up_1: bfloat16 [1024, 3072], P('fsdp')
- w_down_1: bfloat16 [3072, 1024], P('fsdp')
- q_norm_1: float32 [2048], P('fsdp')
- k_norm_1: float32 [1024], P('fsdp')
- ln_gamma_2: float32 [1024], P('fsdp')
- w_q_2: bfloat16 [1024, 2048], P('fsdp')
- w_k_2: bfloat16 [1024, 1024], P('fsdp')
- w_v_2: bfloat16 [1024, 1024], P('fsdp')
- w_o_2: bfloat16 [2048, 1024], P('fsdp')
- w_gate_2: bfloat16 [1024, 3072], P('fsdp')
- w_up_2: bfloat16 [1024, 3072], P('fsdp')
- w_down_2: bfloat16 [3072, 1024], P('fsdp')
- q_norm_2: float32 [2048], P('fsdp')
- k_norm_2: float32 [1024], P('fsdp')
Outputs:
- output 1: bfloat16 [16, 384, 1024], P('fsdp')
- output 2: bfloat16 [16, 384, 1024], P('fsdp')
- output 3: float32 [1024], P('fsdp')
- output 4: float32 [1024, 2048], P('fsdp')
- output 5: float32 [1024, 1024], P('fsdp')
- output 6: float32 [1024, 1024], P('fsdp')
- output 7: float32 [2048, 1024], P('fsdp')
- output 8: float32 [1024, 3072], P('fsdp')
- output 9: float32 [1024, 3072], P('fsdp')
- output 10: float32 [3072, 1024], P('fsdp')
- output 11: float32 [2048], P('fsdp')
- output 12: float32 [1024], P('fsdp')
- output 13: float32 [1024], P('fsdp')
- output 14: float32 [1024, 2048], P('fsdp')
- output 15: float32 [1024, 1024], P('fsdp')
- output 16: float32 [1024, 1024], P('fsdp')
- output 17: float32 [2048, 1024], P('fsdp')
- output 18: float32 [1024, 3072], P('fsdp')
- output 19: float32 [1024, 3072], P('fsdp')
- output 20: float32 [3072, 1024], P('fsdp')
- output 21: float32 [2048], P('fsdp')
- output 22: float32 [1024], P('fsdp')
All inputs are finite; a program needn't handle non-finite values.
Results may differ from a plain program's by a relative error of at most 0.0197592.
Values are sent between devices in bfloat16 or wider.
A program may use at most 1 GiB of HBM per device.

v0:
```python
import functools
import jax
import jax.numpy as jnp
from jax import lax
from jax.sharding import PartitionSpec as P, NamedSharding

HEAD_DIM = 128
EPSILON = 1e-5
ROPE_THETA = 7.5e7
FSDP_AXIS = 'fsdp'


def layer_norm32(values, weight):
    row_mean = jnp.mean(values, axis=-1, keepdims=True)
    centered = values - row_mean
    variance = jnp.mean(centered * centered, axis=-1, keepdims=True)
    return centered * lax.rsqrt(variance + EPSILON) * weight


def rope_tables(positions):
    inv_freq = ROPE_THETA ** (-jnp.arange(0, HEAD_DIM, 2, dtype=jnp.float32) / HEAD_DIM)
    angles = positions.astype(jnp.float32)[:, None] * inv_freq[None, :]
    return jnp.cos(angles), jnp.sin(angles)


def apply_rope(values, cos_tab, sin_tab):
    pair_view = values.reshape(values.shape[:-1] + (HEAD_DIM // 2, 2))
    even_part = pair_view[..., 0]
    odd_part = pair_view[..., 1]
    cos_b = cos_tab[:, None, :]
    sin_b = sin_tab[:, None, :]
    rotated = jnp.stack([even_part * cos_b - odd_part * sin_b, even_part * sin_b + odd_part * cos_b], axis=-1)
    return rotated.reshape(values.shape)


def attention_core(q_raw, k_raw, v_heads, q_norm, k_norm, cos_tab, sin_tab):
    batch_len, seq_len, n_heads = q_raw.shape[0], q_raw.shape[1], q_raw.shape[2]
    n_kv = k_raw.shape[2]
    q_rot = apply_rope(layer_norm32(q_raw, q_norm), cos_tab, sin_tab).astype(jnp.bfloat16)
    k_rot = apply_rope(layer_norm32(k_raw, k_norm), cos_tab, sin_tab).astype(jnp.bfloat16)
    q_grp = q_rot.reshape(batch_len, seq_len, n_kv, n_heads // n_kv, HEAD_DIM)
    scores = jnp.einsum('bqkgd,bskd->bkgqs', q_grp, k_rot, preferred_element_type=jnp.float32) * HEAD_DIM ** -0.5
    causal = jnp.arange(seq_len)[:, None] >= jnp.arange(seq_len)[None, :]
    attn_prob = jax.nn.softmax(jnp.where(causal, scores, -1e30), axis=-1).astype(jnp.bfloat16)
    context = jnp.einsum('bkgqs,bskd->bqkgd', attn_prob, v_heads, preferred_element_type=jnp.float32)
    return context.astype(jnp.bfloat16).reshape(batch_len, seq_len, n_heads * HEAD_DIM)


def swiglu(gate_proj, up_proj):
    return jax.nn.silu(gate_proj) * up_proj


def layer_forward(stream, params, cos_tab, sin_tab):
    ln_gamma, w_q, w_k, w_v, w_o, w_gate, w_up, w_down, q_norm, k_norm = params
    lead_shape = stream.shape[:-1]
    n_heads = w_q.shape[1] // HEAD_DIM
    n_kv = w_k.shape[1] // HEAD_DIM
    x_f32 = stream.astype(jnp.float32)
    normed = layer_norm32(x_f32, ln_gamma).astype(jnp.bfloat16)
    q_raw = jnp.dot(normed, w_q, preferred_element_type=jnp.float32).reshape(lead_shape + (n_heads, HEAD_DIM))
    k_raw = jnp.dot(normed, w_k, preferred_element_type=jnp.float32).reshape(lead_shape + (n_kv, HEAD_DIM))
    v_heads = jnp.dot(normed, w_v, preferred_element_type=jnp.float32).astype(jnp.bfloat16).reshape(lead_shape + (n_kv, HEAD_DIM))
    attn_out = attention_core(q_raw, k_raw, v_heads, q_norm.reshape(n_heads, HEAD_DIM), k_norm.reshape(n_kv, HEAD_DIM), cos_tab, sin_tab)
    gate_proj = jnp.dot(normed, w_gate, preferred_element_type=jnp.float32)
    up_proj = jnp.dot(normed, w_up, preferred_element_type=jnp.float32)
    hidden = swiglu(gate_proj, up_proj).astype(jnp.bfloat16)
    layer_sum = x_f32 + jnp.dot(attn_out, w_o, preferred_element_type=jnp.float32) + jnp.dot(hidden, w_down, preferred_element_type=jnp.float32)
    saved_acts = (stream, normed, q_raw, k_raw, v_heads, attn_out, gate_proj, up_proj, hidden)
    return layer_sum.astype(jnp.bfloat16), saved_acts


def layer_backward(grad_y, saved_acts, params, cos_tab, sin_tab):
    ln_gamma, w_q, w_k, w_v, w_o, w_gate, w_up, w_down, q_norm, k_norm = params
    stream, normed, q_raw, k_raw, v_heads, attn_out, gate_proj, up_proj, hidden = saved_acts
    lead_shape = stream.shape[:-1]
    n_heads = q_raw.shape[-2]
    n_kv = k_raw.shape[-2]
    g_w_down = jnp.einsum('bsf,bsd->fd', hidden, grad_y, preferred_element_type=jnp.float32)
    g_w_o = jnp.einsum('bsn,bsd->nd', attn_out, grad_y, preferred_element_type=jnp.float32)
    d_hidden = jnp.einsum('bsd,fd->bsf', grad_y, w_down, preferred_element_type=jnp.float32)
    swiglu_vjp = jax.vjp(swiglu, gate_proj, up_proj)[1]
    d_gate, d_up = swiglu_vjp(d_hidden)
    d_gate = d_gate.astype(jnp.bfloat16)
    d_up = d_up.astype(jnp.bfloat16)
    g_w_gate = jnp.einsum('bsd,bsf->df', normed, d_gate, preferred_element_type=jnp.float32)
    g_w_up = jnp.einsum('bsd,bsf->df', normed, d_up, preferred_element_type=jnp.float32)
    d_attn = jnp.einsum('bsd,nd->bsn', grad_y, w_o, preferred_element_type=jnp.float32).astype(jnp.bfloat16)
    core_fn = functools.partial(attention_core, cos_tab=cos_tab, sin_tab=sin_tab)
    core_vjp = jax.vjp(core_fn, q_raw, k_raw, v_heads, q_norm.reshape(n_heads, HEAD_DIM), k_norm.reshape(n_kv, HEAD_DIM))[1]
    d_qraw, d_kraw, d_vheads, g_q_norm, g_k_norm = core_vjp(d_attn)
    d_q = d_qraw.astype(jnp.bfloat16).reshape(lead_shape + (n_heads * HEAD_DIM,))
    d_k = d_kraw.astype(jnp.bfloat16).reshape(lead_shape + (n_kv * HEAD_DIM,))
    d_v = d_vheads.reshape(lead_shape + (n_kv * HEAD_DIM,))
    g_w_q = jnp.einsum('bsd,bsn->dn', normed, d_q, preferred_element_type=jnp.float32)
    g_w_k = jnp.einsum('bsd,bsn->dn', normed, d_k, preferred_element_type=jnp.float32)
    g_w_v = jnp.einsum('bsd,bsn->dn', normed, d_v, preferred_element_type=jnp.float32)
    d_normed = (jnp.einsum('bsf,df->bsd', d_gate, w_gate, preferred_element_type=jnp.float32)
                + jnp.einsum('bsf,df->bsd', d_up, w_up, preferred_element_type=jnp.float32)
                + jnp.einsum('bsn,dn->bsd', d_q, w_q, preferred_element_type=jnp.float32)
                + jnp.einsum('bsn,dn->bsd', d_k, w_k, preferred_element_type=jnp.float32)
                + jnp.einsum('bsn,dn->bsd', d_v, w_v, preferred_element_type=jnp.float32))
    norm_vjp = jax.vjp(layer_norm32, stream.astype(jnp.float32), ln_gamma)[1]
    d_stream, g_ln_gamma = norm_vjp(d_normed)
    grad_x = (grad_y.astype(jnp.float32) + d_stream).astype(jnp.bfloat16)
    grads = (g_ln_gamma, g_w_q, g_w_k, g_w_v, g_w_o, g_w_gate, g_w_up, g_w_down, g_q_norm.reshape(-1), g_k_norm.reshape(-1))
    return grad_x, grads


def gather_full(shards):
    return tuple(lax.all_gather(param_piece, FSDP_AXIS, axis=0, tiled=True) for param_piece in shards)


def reduce_shards(grads):
    return tuple(lax.psum_scatter(part_grad, FSDP_AXIS, scatter_dimension=0, tiled=True) for part_grad in grads)


def layer_specs():
    vector_spec = P(FSDP_AXIS)
    matrix_spec = P(FSDP_AXIS, None)
    return (vector_spec,) + (matrix_spec,) * 7 + (vector_spec, vector_spec)


def solution(mesh):
    act_spec = P(FSDP_AXIS, None, None)
    param_spec = layer_specs()
    in_specs = (act_spec, P(), act_spec) + param_spec + param_spec
    out_specs = (act_spec, act_spec) + param_spec + param_spec

    def body(x_in, positions, grad_out, *shards):
        cos_tab, sin_tab = rope_tables(positions)
        half_count = len(shards) // 2
        layer_shards = [shards[:half_count], shards[half_count:]]
        stream = x_in
        saved_list = []
        for layer_params in layer_shards:
            full_params = gather_full(layer_params)
            stream, saved_acts = layer_forward(stream, full_params, cos_tab, sin_tab)
            saved_list.append(saved_acts)
        grad_stream = grad_out
        grad_parts = [None, None]
        for layer_index in (1, 0):
            own_shards, grad_stream, stream = lax.optimization_barrier((layer_shards[layer_index], grad_stream, stream))
            full_params = gather_full(own_shards)
            grad_stream, grads = layer_backward(grad_stream, saved_list[layer_index], full_params, cos_tab, sin_tab)
            grad_parts[layer_index] = reduce_shards(grads)
        return (stream, grad_stream) + grad_parts[0] + grad_parts[1]

    return jax.shard_map(body, mesh=mesh, in_specs=in_specs, out_specs=out_specs, check_vma=False)
```

profile of v0, /device:TPU:0, one launch (start us, length us, event | category | flops | bytes accessed | tf_op | source)
XLA Modules:
  0.0 2326.5 jit_solution(15713137822837211082)
XLA Ops:
  18.0 14.3 all-gather
  34.6 32.4 %all-reduce.25 = (f32[1024]{0:T(1024)S(1)}, f32[1024]{0:T(1024)S(1)}, f32[1024]{0:T(1024)S(1)}, f32[1024]{0:T(1024)S(1)}) all-reduce(f32[1024]{0:T(1024)S(1)} %dynamic-update-slice, f32[1024]{0:T(1024)S(1)} %dynamic-update-slice.1, f32[1024]{0:T(1024)S(1)} %dynamic-update-slice.2, ...), channel_id=1, replica_groups=mesh['fsdp'=16] {'fsdp'}, use_global_device_ids=true, to_apply=%add.8 | all-reduce | flops 4096 | bytes 32768
  67.2 12.5 all-gather.1
  168.6 23.7 %all-gather.41.cloned.1.call-done = bf16[1024,3072]{1,0:T(8,128)(2,1)} async-done(((bf16[64,3072]{1,0:T(8,128)(2,1)}), bf16[1024,3072]{1,0:T(8,128)(2,1)}) %all-gather.41.cloned.1.call-update) | async-done | bytes 6291472 | tf_op jit(solution)/shard_map/all_gather | solution.py:110
  199.5 37.0 %all-gather.43.cloned.1.call-done = bf16[1024,3072]{1,0:T(8,128)(2,1)} async-done(((bf16[64,3072]{1,0:T(8,128)(2,1)}), bf16[1024,3072]{1,0:T(8,128)(2,1)}) %all-gather.43.cloned.1.call-update) | async-done | bytes 6291472 | tf_op jit(solution)/shard_map/all_gather | solution.py:110
  245.3 35.6 %all-gather.45.cloned.1.call-done = bf16[3072,1024]{1,0:T(8,128)(2,1)} async-done(((bf16[192,1024]{1,0:T(8,128)(2,1)}), bf16[3072,1024]{1,0:T(8,128)(2,1)}) %all-gather.45.cloned.1.call-update) | async-done | bytes 6291472 | tf_op jit(solution)/shard_map/all_gather | solution.py:110
  287.5 31.1 %all-gather.51.cloned.1.call-done = bf16[1024,2048]{1,0:T(8,128)(2,1)} async-done(((bf16[64,2048]{1,0:T(8,128)(2,1)}), bf16[1024,2048]{1,0:T(8,128)(2,1)}) %all-gather.51.cloned.1.call-update) | async-done | bytes 4194320 | tf_op jit(solution)/shard_map/all_gather | solution.py:110
  392.5 25.4 %all-gather.53.cloned.1.call-done = bf16[2048,1024]{1,0:T(8,128)(2,1)} async-done(((bf16[128,1024]{1,0:T(8,128)(2,1)}), bf16[2048,1024]{1,0:T(8,128)(2,1)}) %all-gather.53.cloned.1.call-update) | async-done | bytes 4194320 | tf_op jit(solution)/shard_map/all_gather | solution.py:110
  423.5 38.6 %all-gather.55.cloned.1.call-done = bf16[1024,3072]{1,0:T(8,128)(2,1)} async-done(((bf16[64,3072]{1,0:T(8,128)(2,1)}), bf16[1024,3072]{1,0:T(8,128)(2,1)}) %all-gather.55.cloned.1.call-update) | async-done | bytes 6291472 | tf_op jit(solution)/shard_map/all_gather | solution.py:110
  469.3 37.2 %all-gather.57.cloned.1.call-done = bf16[1024,3072]{1,0:T(8,128)(2,1)} async-done(((bf16[64,3072]{1,0:T(8,128)(2,1)}), bf16[1024,3072]{1,0:T(8,128)(2,1)}) %all-gather.57.cloned.1.call-update) | async-done | bytes 6291472 | tf_op jit(solution)/shard_map/all_gather | solution.py:110
  515.5 35.3 %all-gather.59.cloned.1.call-done = bf16[3072,1024]{1,0:T(8,128)(2,1)} async-done(((bf16[192,1024]{1,0:T(8,128)(2,1)}), bf16[3072,1024]{1,0:T(8,128)(2,1)}) %all-gather.59.cloned.1.call-update) | async-done | bytes 6291472 | tf_op jit(solution)/shard_map/all_gather | solution.py:110
  564.6 12.4 all-gather.2
  596.1 31.8 %all-reduce.24 = (f32[1024]{0:T(1024)S(1)}, f32[1024]{0:T(1024)S(1)}) all-reduce(f32[1024]{0:T(1024)S(1)} %dynamic-update-slice.4, f32[1024]{0:T(1024)S(1)} %dynamic-update-slice.5), channel_id=1, replica_groups=mesh['fsdp'=16] {'fsdp'}, use_global_device_ids=true, to_apply=%add.12 | all-reduce | flops 2048 | bytes 16384
  779.2 12.4 multiply_convert_fusion.1
  806.5 19.5 all-gather.73.cloned.1.call-done
  871.1 12.4 all-gather.3
  905.0 31.7 %all-reduce.23 = (f32[1024]{0:T(1024)S(1)}, f32[1024]{0:T(1024)}) all-reduce(f32[1024]{0:T(1024)} %copy-done.147, f32[1024]{0:T(1024)S(1)} %dynamic-update-slice.7), channel_id=1, replica_groups=mesh['fsdp'=16] {'fsdp'}, use_global_device_ids=true, to_apply=%add.14 | all-reduce | flops 2048 | bytes 16384
  1104.9 10.0 multiply_reduce_fusion.1
  1142.5 11.0 multiply_convert_fusion
  1204.0 34.0 %all-reduce.22 = (f32[1024]{0:T(1024)S(1)}, f32[2048]{0:T(1024)S(1)}, f32[1024]{0:T(1024)S(1)}, f32[1024]{0:T(1024)S(1)}, f32[2048]{0:T(1024)S(1)}, /*index=5*/f32[1024]{0:T(1024)S(1)}) all-reduce(f32[1024]{0:T(1024)S(1)} %get-tuple-element.80, f32[2048]{0:T(1024)S(1)} %reshape.1710, ...), channel_id=2, replica_groups=mesh['fsdp'=16] {'fsdp'}, use_global_device_ids=true, to_apply=%region_35.36.clone | all-reduce | flops 8192 | bytes 65536
  1243.0 86.3 %reduce-scatter.35.cloned.1.call-done = f32[128,1024]{1,0:T(8,128)} async-done(((f32[2048,1024]{1,0:T(8,128)}), f32[128,1024]{1,0:T(8,128)}) %reduce-scatter.35.cloned.1.call-update) | async-done | bytes 524304 | tf_op jit(solution)/shard_map/reduce_scatter | solution.py:114
  1329.3 94.6 %reduce-scatter.41.cloned.1.call-done = f32[192,1024]{1,0:T(8,128)} async-done(((f32[3072,1024]{1,0:T(8,128)}), f32[192,1024]{1,0:T(8,128)}) %reduce-scatter.41.cloned.1.call-update) | async-done | bytes 786448 | tf_op jit(solution)/shard_map/reduce_scatter | solution.py:114
  1423.9 95.7 %reduce-scatter.29.cloned.1.call-done = f32[64,2048]{1,0:T(8,128)} async-done(((f32[1024,2048]{1,0:T(8,128)}), f32[64,2048]{1,0:T(8,128)}) %reduce-scatter.29.cloned.1.call-update) | async-done | bytes 524304 | tf_op jit(solution)/shard_map/reduce_scatter | solution.py:114
  1519.6 65.0 %reduce-scatter.17.cloned.1.call-done = f32[64,1024]{1,0:T(8,128)} async-done(((f32[1024,1024]{1,0:T(8,128)}), f32[64,1024]{1,0:T(8,128)}) %reduce-scatter.17.cloned.1.call-update) | async-done | bytes 262160 | tf_op jit(solution)/shard_map/reduce_scatter | solution.py:114
  1584.6 66.2 %reduce-scatter.19.cloned.1.call-done = f32[64,1024]{1,0:T(8,128)} async-done(((f32[1024,1024]{1,0:T(8,128)}), f32[64,1024]{1,0:T(8,128)}) %reduce-scatter.19.cloned.1.call-update) | async-done | bytes 262160 | tf_op jit(solution)/shard_map/reduce_scatter | solution.py:114
  1650.8 94.9 %reduce-scatter.21.cloned.1.call-done = f32[128,1024]{1,0:T(8,128)} async-done(((f32[2048,1024]{1,0:T(8,128)}), f32[128,1024]{1,0:T(8,128)}) %reduce-scatter.21.cloned.1.call-update) | async-done | bytes 524304 | tf_op jit(solution)/shard_map/reduce_scatter | solution.py:114
  1745.7 94.5 %reduce-scatter.27.cloned.1.call-done = f32[192,1024]{1,0:T(8,128)} async-done(((f32[3072,1024]{1,0:T(8,128)}), f32[192,1024]{1,0:T(8,128)}) %reduce-scatter.27.cloned.1.call-update) | async-done | bytes 786448 | tf_op jit(solution)/shard_map/reduce_scatter | solution.py:114
  1840.2 96.4 %reduce-scatter.37.cloned.1.call-done = f32[64,3072]{1,0:T(8,128)} async-done(((f32[1024,3072]{1,0:T(8,128)}), f32[64,3072]{1,0:T(8,128)}) %reduce-scatter.37.cloned.1.call-update) | async-done | bytes 786448 | tf_op jit(solution)/shard_map/reduce_scatter | solution.py:114
  1936.6 96.3 %reduce-scatter.39.cloned.1.call-done = f32[64,3072]{1,0:T(8,128)} async-done(((f32[1024,3072]{1,0:T(8,128)}), f32[64,3072]{1,0:T(8,128)}) %reduce-scatter.39.cloned.1.call-update) | async-done | bytes 786448 | tf_op jit(solution)/shard_map/reduce_scatter | solution.py:114
  2032.9 95.8 %reduce-scatter.15.cloned.1.call-done = f32[64,2048]{1,0:T(8,128)} async-done(((f32[1024,2048]{1,0:T(8,128)}), f32[64,2048]{1,0:T(8,128)}) %reduce-scatter.15.cloned.1.call-update) | async-done | bytes 524304 | tf_op jit(solution)/shard_map/reduce_scatter | solution.py:114
  2128.7 94.7 %reduce-scatter.23.cloned.1.call-done = f32[64,3072]{1,0:T(8,128)} async-done(((f32[1024,3072]{1,0:T(8,128)}), f32[64,3072]{1,0:T(8,128)}) %reduce-scatter.23.cloned.1.call-update) | async-done | bytes 786448 | tf_op jit(solution)/shard_map/reduce_scatter | solution.py:114
  2223.3 96.5 %reduce-scatter.25.cloned.1.call-done = f32[64,3072]{1,0:T(8,128)} async-done(((f32[1024,3072]{1,0:T(8,128)}), f32[64,3072]{1,0:T(8,128)}) %reduce-scatter.25.cloned.1.call-update) | async-done | bytes 786448 | tf_op jit(solution)/shard_map/reduce_scatter | solution.py:114
  (701 shorter events, 734.9 us)
Async XLA Ops:
  11.2 269.8 %all-gather.45.cloned.1.call-start = ((), (), s32[]{:S(2)}) async-start(), calls=%async_computation.20 | async-start | bytes 6684672 | tf_op jit(solution)/shard_map/all_gather | solution.py:110
  11.9 306.7 %all-gather.51.cloned.1.call-start = ((), (), s32[]{:S(2)}) async-start(), calls=%async_computation.23 | async-start | bytes 4456448 | tf_op jit(solution)/shard_map/all_gather | solution.py:110
  12.7 347.0 %all-gather.49.cloned.1.call-start = ((), (), s32[]{:S(2)}) async-start(), calls=%async_computation.22 | async-start | bytes 2228224 | tf_op jit(solution)/shard_map/all_gather | solution.py:110
  13.5 366.9 %all-gather.47.cloned.1.call-start = ((), (), s32[]{:S(2)}) async-start(), calls=%async_computation.21 | async-start | bytes 2228224 | tf_op jit(solution)/shard_map/all_gather | solution.py:110
  14.1 403.8 %all-gather.53.cloned.1.call-start = ((), (), s32[]{:S(2)}) async-start(), calls=%async_computation.24 | async-start | bytes 4456448 | tf_op jit(solution)/shard_map/all_gather | solution.py:110
  14.8 447.3 %all-gather.55.cloned.1.call-start = ((), (), s32[]{:S(2)}) async-start(), calls=%async_computation.25 | async-start | bytes 6684672 | tf_op jit(solution)/shard_map/all_gather | solution.py:110
  15.4 491.1 %all-gather.57.cloned.1.call-start = ((), (), s32[]{:S(2)}) async-start(), calls=%async_computation.26 | async-start | bytes 6684672 | tf_op jit(solution)/shard_map/all_gather | solution.py:110
  16.1 534.6 %all-gather.59.cloned.1.call-start = ((), (), s32[]{:S(2)}) async-start(), calls=%async_computation.27 | async-start | bytes 6684672 | tf_op jit(solution)/shard_map/all_gather | solution.py:110
  16.7 629.3 %all-gather.67.cloned.1.call-start = ((), (), s32[]{:S(2)}) async-start(), calls=%async_computation.31 | async-start | bytes 4456448 | tf_op jit(solution)/shard_map/all_gather | solution.py:110
  560.7 238.4 %all-gather.65.cloned.1.call-start = ((), (), s32[]{:S(2)}) async-start(), calls=%async_computation.30 | async-start | bytes 6684672 | tf_op jit(solution)/shard_map/all_gather | solution.py:110
  561.3 264.7 %all-gather.73.cloned.1.call-start = ((), (), s32[]{:S(2)}) async-start(), calls=%async_computation.34 | async-start | bytes 2228224 | tf_op jit(solution)/shard_map/all_gather | solution.py:110
  645.9 308.5 %all-gather.81.cloned.1.call-start = ((), (), s32[]{:S(2)}) async-start(), calls=%async_computation.38 | async-start | bytes 4456448 | tf_op jit(solution)/shard_map/all_gather | solution.py:110
  832.8 308.6 %all-gather.75.cloned.1.call-start = ((), (), s32[]{:S(2)}) async-start(), calls=%async_computation.35 | async-start | bytes 6684672 | tf_op jit(solution)/shard_map/all_gather | solution.py:110
  833.5 340.6 %all-gather.85.cloned.1.call-start = ((), (), s32[]{:S(2)}) async-start(), calls=%async_computation.40 | async-start | bytes 2228224 | tf_op jit(solution)/shard_map/all_gather | solution.py:110
  834.1 344.1 %all-gather.83.cloned.1.call-start = ((), (), s32[]{:S(2)}) async-start(), calls=%async_computation.39 | async-start | bytes 4456448 | tf_op jit(solution)/shard_map/all_gather | solution.py:110
  834.9 348.5 %all-gather.77.cloned.1.call-start = ((), (), s32[]{:S(2)}) async-start(), calls=%async_computation.36 | async-start | bytes 6684672 | tf_op jit(solution)/shard_map/all_gather | solution.py:110
  835.4 355.3 %all-gather.79.cloned.1.call-start = ((), (), s32[]{:S(2)}) async-start(), calls=%async_computation.37 | async-start | bytes 6684672 | tf_op jit(solution)/shard_map/all_gather | solution.py:110
  836.0 362.0 %all-gather.87.cloned.1.call-start = ((), (), s32[]{:S(2)}) async-start(), calls=%async_computation.41 | async-start | bytes 2228224 | tf_op jit(solution)/shard_map/all_gather | solution.py:110
  836.8 406.2 %reduce-scatter.31.cloned.1.call-start = ((), (), s32[]{:S(2)}) async-start(), calls=%async_computation.50 | async-start | bytes 4456448 | tf_op jit(solution)/shard_map/reduce_scatter | solution.py:114
  840.3 402.7 %reduce-scatter.33.cloned.1.call-start = ((), (), s32[]{:S(2)}) async-start(), calls=%async_computation.51 | async-start | bytes 4456448 | tf_op jit(solution)/shard_map/reduce_scatter | solution.py:114
  845.0 484.3 %reduce-scatter.35.cloned.1.call-start = ((), (), s32[]{:S(2)}) async-start(), calls=%async_computation.52 | async-start | bytes 8912896 | tf_op jit(solution)/shard_map/reduce_scatter | solution.py:114
  853.3 570.7 %reduce-scatter.41.cloned.1.call-start = ((), (), s32[]{:S(2)}) async-start(), calls=%async_computation.55 | async-start | bytes 13369344 | tf_op jit(solution)/shard_map/reduce_scatter | solution.py:114
  861.4 658.2 %reduce-scatter.29.cloned.1.call-start = ((), (), s32[]{:S(2)}) async-start(), calls=%async_computation.49 | async-start | bytes 8912896 | tf_op jit(solution)/shard_map/reduce_scatter | solution.py:114
  868.8 715.8 %reduce-scatter.17.cloned.1.call-start = ((), (), s32[]{:S(2)}) async-start(), calls=%async_computation.43 | async-start | bytes 4456448 | tf_op jit(solution)/shard_map/reduce_scatter | solution.py:114
  1019.2 631.5 %reduce-scatter.19.cloned.1.call-start = ((), (), s32[]{:S(2)}) async-start(), calls=%async_computation.44 | async-start | bytes 4456448 | tf_op jit(solution)/shard_map/reduce_scatter | solution.py:114
  1030.7 715.0 %reduce-scatter.21.cloned.1.call-start = ((), (), s32[]{:S(2)}) async-start(), calls=%async_computation.45 | async-start | bytes 8912896 | tf_op jit(solution)/shard_map/reduce_scatter | solution.py:114
  1038.9 801.3 %reduce-scatter.27.cloned.1.call-start = ((), (), s32[]{:S(2)}) async-start(), calls=%async_computation.48 | async-start | bytes 13369344 | tf_op jit(solution)/shard_map/reduce_scatter | solution.py:114
  1047.3 889.3 %reduce-scatter.37.cloned.1.call-start = ((), (), s32[]{:S(2)}) async-start(), calls=%async_computation.53 | async-start | bytes 13369344 | tf_op jit(solution)/shard_map/reduce_scatter | solution.py:114
  1056.6 976.3 %reduce-scatter.39.cloned.1.call-start = ((), (), s32[]{:S(2)}) async-start(), calls=%async_computation.54 | async-start | bytes 13369344 | tf_op jit(solution)/shard_map/reduce_scatter | solution.py:114
  1065.0 1063.7 %reduce-scatter.15.cloned.1.call-start = ((), (), s32[]{:S(2)}) async-start(), calls=%async_computation.42 | async-start | bytes 8912896 | tf_op jit(solution)/shard_map/reduce_scatter | solution.py:114
  1141.3 1082.0 %reduce-scatter.23.cloned.1.call-start = ((), (), s32[]{:S(2)}) async-start(), calls=%async_computation.46 | async-start | bytes 13369344 | tf_op jit(solution)/shard_map/reduce_scatter | solution.py:114
  1161.6 1158.2 %reduce-scatter.25.cloned.1.call-start = ((), (), s32[]{:S(2)}) async-start(), calls=%async_computation.47 | async-start | bytes 13369344 | tf_op jit(solution)/shard_map/reduce_scatter | solution.py:114
  (173 other events, 3913.4 us)
Sparse Core Ops, SparseCore 0:
  75.0 35.4 all-gather.36
  112.6 35.3 all-gather.38
  150.1 42.1 all-gather.40
  194.4 42.1 all-gather.42
  238.8 42.1 all-gather.44
  283.2 35.3 all-gather.50
  382.4 35.3 all-gather.52
  419.9 42.1 all-gather.54
  464.3 42.1 all-gather.56
  508.6 42.1 all-gather.58
  558.3 35.3 all-gather.66
  626.8 35.3 all-gather.68
  664.3 42.1 all-gather.60
  708.7 42.1 all-gather.62
  752.9 42.1 all-gather.64
  870.6 42.3 all-gather.74
  983.7 42.1 all-gather.76
  1028.0 42.1 all-gather.78
  1103.8 63.9 reduce-scatter.30
  1170.5 63.2 reduce-scatter.32
  1236.7 92.5 reduce-scatter.34
  1334.5 89.3 reduce-scatter.40
  1426.6 92.9 reduce-scatter.28
  1522.4 62.1 reduce-scatter.16
  1587.5 63.2 reduce-scatter.18
  1653.5 92.1 reduce-scatter.20
  1750.7 89.3 reduce-scatter.26
  1845.4 91.1 reduce-scatter.36
  1941.6 91.1 reduce-scatter.38
  2035.7 92.9 reduce-scatter.14
  2133.9 89.4 reduce-scatter.22
  2228.6 91.2 reduce-scatter.24
  (10 shorter events, 302.3 us)
where the time goes:
time: 2340 us; the launch traced here: 2330 us
  waiting for transfers between devices  1380 us (59%)
  matrix products  340 us (15%)
  local copies, waits for them, and re-layouts  220 us (9%)
  other arithmetic  185 us (8%)
  blocking collectives  181 us (8%)
    reduce_scatter x14, waiting for transfers between devices, reduce_shards(): lax.psum_scatter(part_grad, FSDP_AXIS, scatter_dimension=0, tiled=True)  1080 us
    all_gather x28, waiting for transfers between devices, gather_full(): lax.all_gather(param_piece, FSDP_AXIS, axis=0, tiled=True)  289 us
    unnamed x4, blocking collectives  130 us
    unnamed x354, local copies, waits for them, and re-layouts  57.2 us
    all_gather x4, blocking collectives, gather_full(): lax.all_gather(param_piece, FSDP_AXIS, axis=0, tiled=True)  51.6 us
  transfers between devices with their start and end apart: 42, of which 22 were waited for; matrix products, arithmetic and copies ran while one was open for 30% of the time, Pallas kernels for 0%

commit v1 on v0

v1 whole, which is shorter than its diff:
```python
import jax
import jax.numpy as jnp
from jax import lax
from jax.experimental import pallas as pl
from jax.experimental.pallas import tpu as pltpu
from jax.sharding import Mesh, PartitionSpec as P


HEAD_DIM = 128
EPSILON = 1e-5
ROPE_THETA = 7.5e7
AX = ('z', 'y', 'x', 'c')
CHIP_AXES = ('z', 'y', 'x')
BIT = {'z': 4, 'y': 2, 'x': 1}
SWAP = [(0, 1), (1, 0)]
F32 = jnp.float32
BF16 = jnp.bfloat16


def layer_norm32(values, weight):
    row_mean = jnp.mean(values, axis=-1, keepdims=True)
    centered = values - row_mean
    variance = jnp.mean(centered * centered, axis=-1, keepdims=True)
    return centered * lax.rsqrt(variance + EPSILON) * weight


def rope_tables(positions):
    inv_freq = ROPE_THETA ** (-jnp.arange(0, HEAD_DIM, 2, dtype=F32) / HEAD_DIM)
    angles = positions.astype(F32)[:, None] * inv_freq[None, :]
    cos_tab, sin_tab = jnp.cos(angles), jnp.sin(angles)
    cos_full = jnp.repeat(cos_tab, 2, axis=1)
    sin_full = jnp.stack([-sin_tab, sin_tab], axis=-1).reshape(cos_full.shape)
    return cos_full, sin_full


def swap_pairs(values):
    lane = lax.broadcasted_iota(jnp.int32, values.shape, 1)
    return jnp.where((lane & 1) == 0, pltpu.roll(values, HEAD_DIM - 1, 1), pltpu.roll(values, 1, 1))


def head_stats(values):
    centered = values - jnp.mean(values, axis=-1, keepdims=True)
    scale = lax.rsqrt(jnp.mean(centered * centered, axis=-1, keepdims=True) + EPSILON)
    return centered * scale, scale


def rotate(values, cos_full, sin_full):
    return (values * cos_full + swap_pairs(values) * sin_full).astype(BF16)


def contract(a, b, dim_a, dim_b):
    return lax.dot_general(a, b, (((dim_a,), (dim_b,)), ((), ())), preferred_element_type=F32)


def softmax_rows(q_rot, k_rot):
    scores = contract(q_rot, k_rot, 1, 1) * HEAD_DIM ** -0.5
    row = lax.broadcasted_iota(jnp.int32, scores.shape, 0)
    col = lax.broadcasted_iota(jnp.int32, scores.shape, 1)
    scores = jnp.where(row >= col, scores, -1e30)
    expo = jnp.exp(scores - jnp.max(scores, axis=-1, keepdims=True))
    return expo / jnp.sum(expo, axis=-1, keepdims=True)


def attn_fwd_kernel(q_ref, k_ref, v_ref, qn_ref, kn_ref, cos_ref, sin_ref, o_ref):
    cos_full, sin_full = cos_ref[...], sin_ref[...]
    k_hat, _ = head_stats(k_ref[...])
    k_rot = rotate(k_hat * kn_ref[0], cos_full, sin_full)
    v_head = v_ref[...].astype(BF16)
    for g in range(q_ref.shape[1] // HEAD_DIM):
        cols = slice(g * HEAD_DIM, (g + 1) * HEAD_DIM)
        q_hat, _ = head_stats(q_ref[:, cols])
        q_rot = rotate(q_hat * qn_ref[0, g:g + 1], cos_full, sin_full)
        prob = softmax_rows(q_rot, k_rot).astype(BF16)
        o_ref[:, cols] = contract(prob, v_head, 1, 0).astype(BF16)


def norm_bwd(d_rot, hat, scale, weight, cos_full, sin_full):
    d_val = d_rot.astype(BF16).astype(F32)
    d_out = d_val * cos_full + swap_pairs(d_val * sin_full)
    g_weight = jnp.sum(d_out * hat, axis=0, keepdims=True)
    d_hat = d_out * weight
    mean_d = jnp.mean(d_hat, axis=-1, keepdims=True)
    mean_dh = jnp.mean(d_hat * hat, axis=-1, keepdims=True)
    return (scale * (d_hat - mean_d - hat * mean_dh)).astype(BF16), g_weight


def attn_bwd_kernel(q_ref, k_ref, v_ref, do_ref, qn_ref, kn_ref, cos_ref, sin_ref, dqkv_ref, gq_ref, gk_ref):
    head = pl.program_id(0)
    n_kv = pl.num_programs(0)
    group = q_ref.shape[1] // HEAD_DIM
    cos_full, sin_full = cos_ref[...], sin_ref[...]
    k_hat, k_scale = head_stats(k_ref[...])
    k_rot = rotate(k_hat * kn_ref[0], cos_full, sin_full)
    v_head = v_ref[...].astype(BF16)
    dv = jnp.zeros(v_head.shape, F32)
    dk = jnp.zeros(v_head.shape, F32)
    for g in range(group):
        cols = slice(g * HEAD_DIM, (g + 1) * HEAD_DIM)
        q_hat, q_scale = head_stats(q_ref[:, cols])
        q_rot = rotate(q_hat * qn_ref[0, g:g + 1], cos_full, sin_full)
        prob = softmax_rows(q_rot, k_rot)
        d_out = do_ref[:, cols]
        dv = dv + contract(prob.astype(BF16), d_out, 0, 0)
        d_prob = contract(d_out, v_head, 1, 1).astype(BF16).astype(F32)
        d_score = prob * (d_prob - jnp.sum(d_prob * prob, axis=-1, keepdims=True))
        d_score = (d_score * HEAD_DIM ** -0.5).astype(BF16)
        dk = dk + contract(d_score, q_rot, 0, 0)
        dq, g_q = norm_bwd(contract(d_score, k_rot, 1, 0), q_hat, q_scale, qn_ref[0, g:g + 1], cos_full, sin_full)
        dqkv_ref[:, pl.ds(pl.multiple_of((head * group + g) * HEAD_DIM, HEAD_DIM), HEAD_DIM)] = dq
        gq_ref[0, g:g + 1] = g_q
    dk_raw, g_k = norm_bwd(dk, k_hat, k_scale, kn_ref[0], cos_full, sin_full)
    base = n_kv * group + head
    dqkv_ref[:, pl.ds(pl.multiple_of(base * HEAD_DIM, HEAD_DIM), HEAD_DIM)] = dk_raw
    dqkv_ref[:, pl.ds(pl.multiple_of((base + n_kv) * HEAD_DIM, HEAD_DIM), HEAD_DIM)] = dv.astype(BF16)
    gk_ref[0] = g_k


def qkv_specs(seq_len, n_kv, group):
    q_spec = pl.BlockSpec((seq_len, group * HEAD_DIM), lambda j: (0, j))
    k_spec = pl.BlockSpec((seq_len, HEAD_DIM), lambda j: (0, n_kv * group + j))
    v_spec = pl.BlockSpec((seq_len, HEAD_DIM), lambda j: (0, n_kv * group + n_kv + j))
    qn_spec = pl.BlockSpec((1, group, HEAD_DIM), lambda j: (j, 0, 0))
    kn_spec = pl.BlockSpec((1, 1, HEAD_DIM), lambda j: (j, 0, 0))
    tab_spec = pl.BlockSpec((seq_len, HEAD_DIM), lambda j: (0, 0))
    return q_spec, k_spec, v_spec, qn_spec, kn_spec, tab_spec


def attention_fwd(qkv, q_norm, k_norm, cos_full, sin_full):
    seq_len, n_kv, group = qkv.shape[0], k_norm.shape[0], q_norm.shape[1]
    q_spec, k_spec, v_spec, qn_spec, kn_spec, tab_spec = qkv_specs(seq_len, n_kv, group)
    return pl.pallas_call(
        attn_fwd_kernel,
        grid=(n_kv,),
        in_specs=[q_spec, k_spec, v_spec, qn_spec, kn_spec, tab_spec, tab_spec],
        out_specs=q_spec,
        out_shape=jax.ShapeDtypeStruct((seq_len, n_kv * group * HEAD_DIM), BF16),
        cost_estimate=pl.CostEstimate(flops=1_500_000_000, bytes_accessed=12_000_000, transcendentals=0),
        name='attn_fwd',
    )(qkv, qkv, qkv, q_norm, k_norm, cos_full, sin_full)


def attention_bwd(qkv, d_attn, q_norm, k_norm, cos_full, sin_full):
    seq_len, n_kv, group = qkv.shape[0], k_norm.shape[0], q_norm.shape[1]
    q_spec, k_spec, v_spec, qn_spec, kn_spec, tab_spec = qkv_specs(seq_len, n_kv, group)
    return pl.pallas_call(
        attn_bwd_kernel,
        grid=(n_kv,),
        in_specs=[q_spec, k_spec, v_spec, q_spec, qn_spec, kn_spec, tab_spec, tab_spec],
        out_specs=[pl.BlockSpec(qkv.shape, lambda j: (0, 0)), qn_spec, kn_spec],
        out_shape=[jax.ShapeDtypeStruct(qkv.shape, BF16), jax.ShapeDtypeStruct(q_norm.shape, F32), jax.ShapeDtypeStruct(k_norm.shape, F32)],
        cost_estimate=pl.CostEstimate(flops=4_000_000_000, bytes_accessed=15_000_000, transcendentals=0),
        name='attn_bwd',
    )(qkv, qkv, qkv, d_attn, q_norm, k_norm, cos_full, sin_full)


def swiglu(gate_proj, up_proj):
    return jax.nn.silu(gate_proj) * up_proj


def dot32(a, b):
    return jnp.dot(a, b, preferred_element_type=F32)


def dot_t32(a, b):
    return lax.dot_general(a, b, (((1,), (1,)), ((), ())), preferred_element_type=F32)


def swap_cores(value):
    return lax.ppermute(value, 'c', SWAP)


def pair_rows(act, block_rows, chip_pos, core):
    act_t = act.T
    tokens = act_t.shape[1]

    def pick(which):
        parts = []
        for delta in range(8):
            chip = 0
            for axis in CHIP_AXES:
                chip = chip + BIT[axis] * (chip_pos[axis] ^ (1 if delta & BIT[axis] else 0))
            start = (chip * 2 + which) * block_rows
            parts.append(lax.dynamic_slice(act_t, (start, 0), (block_rows, tokens)))
        return jnp.concatenate(parts, axis=0)

    mine = pick(core)
    theirs = swap_cores(pick(1 - core))
    both = jnp.concatenate([mine, theirs], axis=1)
    return [both[d * block_rows:(d + 1) * block_rows] for d in range(8)]


def pair_tokens(cot):
    pair = lax.optimization_barrier((cot, swap_cores(cot)))
    return jnp.concatenate(pair, axis=0)


def hop(value, axis):
    return lax.ppermute(value, axis, SWAP)


def reduce_group(blocks, cot, dims):
    rows = blocks[0].shape[0]

    def part(b1, b2, b3):
        return blocks[b1 * BIT[dims[0]] + b2 * BIT[dims[1]] + b3 * BIT[dims[2]]]

    send1 = dot32(jnp.concatenate([part(1, 0, 0), part(1, 0, 1), part(1, 1, 0), part(1, 1, 1)], axis=0), cot)
    got1 = hop(send1, dims[0])
    send2 = dot32(jnp.concatenate([part(0, 1, 0), part(0, 1, 1)], axis=0), cot) + got1[2 * rows:]
    got2 = hop(send2, dims[1])
    send3 = dot32(part(0, 0, 1), cot) + got1[rows:2 * rows] + got2[rows:]
    got3 = hop(send3, dims[2])
    return dot32(part(0, 0, 0), cot) + got1[:rows] + got2[:rows] + got3


def scatter_small(values, chip_pos, core):
    value = values.reshape((2, 2, 2, 2) + values.shape[1:])
    for axis, pos in (('c', core), ('x', chip_pos['x']), ('y', chip_pos['y']), ('z', chip_pos['z'])):
        dim = {'z': 0, 'y': 1, 'x': 2, 'c': 3}[axis]
        keep = lax.dynamic_index_in_dim(value, pos, dim, keepdims=False)
        send = lax.dynamic_index_in_dim(value, 1 - pos, dim, keepdims=False)
        value = keep + lax.ppermute(send, axis, SWAP)
    return value


RING = {
    'o': ('z', 'x', 'y'),
    'down': ('x', 'y', 'z'),
    'gate': ('y', 'z', 'x'),
    'up': ('z', 'x', 'y'),
    'q': ('x', 'y', 'z'),
    'kv': ('y', 'z', 'x'),
}


def layer_specs():
    vector_spec = P(AX)
    matrix_spec = P(AX, None)
    return (vector_spec,) + (matrix_spec,) * 7 + (vector_spec, vector_spec)


def solution(mesh):
    cube = Mesh(mesh.devices.reshape(2, 2, 2, 2), AX)
    act_spec = P(AX, None, None)
    param_spec = layer_specs()
    in_specs = (act_spec, P(), act_spec) + param_spec + param_spec
    out_specs = (act_spec, act_spec) + param_spec + param_spec

    def inner(x_in, positions, grad_out, *shards):
        layer_shards = [shards[:10], shards[10:]]
        chip_pos = {axis: lax.axis_index(axis) for axis in CHIP_AXES}
        core = lax.axis_index('c')

        def gather(piece):
            return lax.all_gather(piece, AX, axis=0, tiled=True)

        cos_full, sin_full = rope_tables(positions)

        weights = []
        for _, w_q, w_k, w_v, w_o, w_gate, w_up, w_down, _, _ in layer_shards:
            w_in = gather(jnp.concatenate([w_q, w_k, w_v, w_gate, w_up], axis=1))
            qkv_width = w_q.shape[1] + w_k.shape[1] + w_v.shape[1]
            w_qkv, w_gu = w_in[:, :qkv_width], w_in[:, qkv_width:]
            w_od = gather(jnp.concatenate([w_o, w_down], axis=0))
            rows_o, rows_d = w_o.shape[0], w_down.shape[0]
            w_od = w_od.reshape(16, rows_o + rows_d, -1)
            weights.append((w_qkv, w_gu, w_od[:, :rows_o].reshape(16 * rows_o, -1), w_od[:, rows_o:].reshape(16 * rows_d, -1)))
        vecs = jnp.concatenate([v for s in layer_shards for v in (s[0], s[8], s[9])])
        vec_sizes = [v.shape[0] for s in layer_shards for v in (s[0], s[8], s[9])]
        vecs = lax.all_gather(vecs, AX, axis=0, tiled=False)
        small, offset = [], 0
        for size in vec_sizes:
            small.append(vecs[:, offset:offset + size].reshape(-1))
            offset += size

        stream = x_in[0]
        saved = []
        for layer in range(2):
            w_qkv, w_gu, w_o_full, w_down_full = weights[layer]
            ln_gamma = small[3 * layer]
            n_kv = small[3 * layer + 2].shape[0] // HEAD_DIM
            q_norm = small[3 * layer + 1].reshape(n_kv, -1, HEAD_DIM)
            k_norm = small[3 * layer + 2].reshape(n_kv, 1, HEAD_DIM)
            q_width, kv_width = q_norm.size, k_norm.size
            x_f32 = stream.astype(F32)
            normed32, norm_vjp = jax.vjp(layer_norm32, x_f32, ln_gamma)
            normed = normed32.astype(BF16)
            qkv = dot32(normed, w_qkv)
            attn_out = attention_fwd(qkv, q_norm, k_norm, cos_full, sin_full)
            gate_up = dot32(normed, w_gu)
            ffn = gate_up.shape[1] // 2
            hidden32, swiglu_vjp = jax.vjp(swiglu, gate_up[:, :ffn], gate_up[:, ffn:])
            hidden = hidden32.astype(BF16)
            layer_sum = x_f32 + dot32(attn_out, w_o_full) + dot32(hidden, w_down_full)
            stream = layer_sum.astype(BF16)
            saved.append((norm_vjp, normed, qkv, q_norm, k_norm, attn_out, swiglu_vjp, hidden, q_width, kv_width))

        grad = grad_out[0]
        out_grads = [None, None]
        small_grads = [None, None]
        for layer in (1, 0):
            norm_vjp, normed, qkv, q_norm, k_norm, attn_out, swiglu_vjp, hidden, q_width, kv_width = saved[layer]
            w_qkv, w_gu, w_o_full, w_down_full = weights[layer]
            ffn = hidden.shape[1]
            grad2 = pair_tokens(grad)
            attn_rows = pair_rows(attn_out, attn_out.shape[1] // 16, chip_pos, core)
            g_o = reduce_group(attn_rows, grad2, RING['o'])
            hidden_rows = pair_rows(hidden, ffn // 16, chip_pos, core)
            g_down = reduce_group(hidden_rows, grad2, RING['down'])
            d_hidden = dot_t32(grad, w_down_full)
            d_gate, d_up = swiglu_vjp(d_hidden)
            d_gu = jnp.concatenate([d_gate.astype(BF16), d_up.astype(BF16)], axis=1)
            normed_rows = pair_rows(normed, normed.shape[1] // 16, chip_pos, core)
            d_gu2 = pair_tokens(d_gu)
            g_gate = reduce_group(normed_rows, d_gu2[:, :ffn], RING['gate'])
            g_up = reduce_group(normed_rows, d_gu2[:, ffn:], RING['up'])
            d_attn = dot_t32(grad, w_o_full).astype(BF16)
            d_qkv, g_q_norm, g_k_norm = attention_bwd(qkv, d_attn, q_norm, k_norm, cos_full, sin_full)
            d_qkv2 = pair_tokens(d_qkv)
            g_q = reduce_group(normed_rows, d_qkv2[:, :q_width], RING['q'])
            g_kv = reduce_group(normed_rows, d_qkv2[:, q_width:], RING['kv'])
            d_normed = dot_t32(d_gu, w_gu) + dot_t32(d_qkv, w_qkv)
            d_stream, g_ln = norm_vjp(d_normed)
            grad = (grad.astype(F32) + d_stream).astype(BF16)
            small_grads[layer] = jnp.concatenate([g_ln.reshape(16, -1), g_q_norm.reshape(16, -1), g_k_norm.reshape(16, -1)], axis=1)
            out_grads[layer] = (g_q, g_kv[:, :kv_width], g_kv[:, kv_width:], g_o, g_gate, g_up, g_down)
        small_sum = scatter_small(jnp.concatenate(small_grads, axis=1), chip_pos, core)
        pieces, offset = [], 0
        for size in vec_sizes:
            pieces.append(small_sum[offset:offset + size])
            offset += size
        outs = []
        for layer in range(2):
            outs += [pieces[3 * layer], *out_grads[layer], pieces[3 * layer + 1], pieces[3 * layer + 2]]
        return (stream[None], grad[None], *outs)

    return jax.shard_map(inner, mesh=cube, in_specs=in_specs, out_specs=out_specs, check_vma=False)
```

time: 2340 us -> 1420 us (0.61)
  waiting for transfers between devices: 1380 us -> 855 us
  blocking collectives: 181 us -> 14.2 us
  other arithmetic: 185 us -> 35.5 us
  local copies, waits for them, and re-layouts: 220 us -> 113 us
  matrix products: 340 us -> 237 us
  Pallas kernels: 0 us -> 101 us
  starting transfers between devices: 2.06 us -> 41.6 us
    reduce_scatter x14 -> x0, waiting for transfers between devices: 1080 us -> none  [reduce_shards(): lax.psum_scatter(part_grad, FSDP_AXIS, scatter_dimension=0, tiled=True)]
    ppermute x0 -> x52, waiting for transfers between devices: none -> 658 us  [the longest x36 656 us: hop(): return lax.ppermute(value, axis, SWAP)]
    unnamed x4 -> x0, blocking collectives: 130 us -> none
    dot_general x56 -> x64, matrix products: 340 us -> 237 us  [the longest x56 168 us: dot32(): return jnp.dot(a, b, preferred_element_type=F32)]
    pallas_call x0 -> x4, Pallas kernels: none -> 101 us  [the longest x2 62.5 us: attention_bwd(): pl.pallas_call(attn_bwd_kernel, grid=(n_kv,), in_specs=[q_spec, k_spec, v...]
    all_gather x28 -> x4, waiting for transfers between devices: 289 us -> 198 us  [gather(): return lax.all_gather(piece, AX, axis=0, tiled=True)]
    reshape x24 -> x4, local copies, waits for them, and re-layouts: 73.9 us -> 1.9 us  [the longest x2 0.95 us: rope_tables(): cos_full = jnp.repeat(cos_tab, 2, axis=1)]
    another operation x16 -> x1, other arithmetic: 49.4 us -> 0.02 us  [rope_tables(): sin_full = jnp.stack([-sin_tab, sin_tab], axis=-1).reshape(cos_full.shape)]
  transfers between devices with their start and end apart: 42 -> 56, of which waited for: 22 -> 27; matrix products, arithmetic and copies ran while one was open for 30% -> 22% of each run, Pallas kernels for 0% -> 4%
where the time goes in v1:
time: 1420 us; the launch traced here: 1410 us
  waiting for transfers between devices  855 us (60%)
  matrix products  237 us (17%)
  local copies, waits for them, and re-layouts  113 us (8%)
  Pallas kernels  101 us (7%)
  starting transfers between devices  41.6 us (3%)
  other arithmetic  35.5 us (2%)
  between operations  15.9 us (1%)
    ppermute x36, waiting for transfers between devices, hop(): return lax.ppermute(value, axis, SWAP)  656 us
    all_gather x4, waiting for transfers between devices, gather(): return lax.all_gather(piece, AX, axis=0, tiled=True)  198 us
    dot_general x56, matrix products, dot32(): return jnp.dot(a, b, preferred_element_type=F32)  168 us
    dot_general x8, matrix products, dot_t32(): lax.dot_general(a, b, (((1,), (1,)), ((), ())), preferred_element_type=F32)  69.1 us
    pallas_call x2, Pallas kernels, attention_bwd(): pl.pallas_call(attn_bwd_kernel, grid=(n_kv,), in_specs=[q_spec, k_spec, v...  62.5 us
    unnamed x302, local copies, waits for them, and re-layouts  39.3 us
    pallas_call x2, Pallas kernels, attention_fwd(): pl.pallas_call(attn_fwd_kernel, grid=(n_kv,), in_specs=[q_spec, k_spec, v...  38.8 us
    ppermute x36, starting transfers between devices, hop(): return lax.ppermute(value, axis, SWAP)  34.4 us
  transfers between devices with their start and end apart: 56, of which 27 were waited for; matrix products, arithmetic and copies ran while one was open for 22% of the time, Pallas kernels for 4%

profile of v1, /device:TPU:0, one launch (start us, length us, event | category | flops | bytes accessed | tf_op | source)
XLA Modules:
  0.0 1414.1 jit_solution(1614778445586518999)
XLA Ops:
  18.4 14.2 %all-gather.1 = f32[16,1,512]{2,1,0:T(1,128)S(1)} all-gather(f32[1,1,512]{2,1,0:T(1,128)S(1)} %bitcast.371), channel_id=2, replica_groups=mesh['z'=2,'y'=2,'x'=2,'c'=2] {'z','y','x','c'}, dimensions={0}, use_global_device_ids=true | all-gather | bytes 34816 | tf_op jit(solution)/shard_map/all_gather | solution.py:270
  40.7 28.9 %all-gather.9.cloned.1.call-done = bf16[5120,1024]{1,0:T(8,128)(2,1)} async-done(((bf16[320,1024]{1,0:T(8,128)(2,1)}), bf16[5120,1024]{1,0:T(8,128)(2,1)}) %all-gather.9.cloned.1.call-update) | async-done | bytes 10485776 | tf_op jit(solution)/shard_map/all_gather | solution.py:255
  81.0 47.3 %all-gather.13.cloned.1.call-done = bf16[5120,1024]{1,0:T(8,128)(2,1)} async-done(((bf16[320,1024]{1,0:T(8,128)(2,1)}), bf16[5120,1024]{1,0:T(8,128)(2,1)}) %all-gather.13.cloned.1.call-update) | async-done | bytes 10485776 | tf_op jit(solution)/shard_map/all_gather | solution.py:255
  143.0 77.7 %all-gather.7.cloned.1.call-done = bf16[1024,10240]{1,0:T(8,128)(2,1)} async-done(((bf16[64,10240]{1,0:T(8,128)(2,1)}), bf16[1024,10240]{1,0:T(8,128)(2,1)}) %all-gather.7.cloned.1.call-update) | async-done | bytes 20971536 | tf_op jit(solution)/shard_map/all_gather | solution.py:255
  220.7 8.9 fusion.14.q_ref.k_ref.v_ref
  229.6 19.3 %attn_fwd.2 = bf16[384,2048]{1,0:T(8,128)(2,1)} custom-call(f32[384,4096]{1,0:T(8,128)} %fusion.14.q_ref.k_ref.v_ref, f32[384,4096]{1,0:T(8,128)} %fusion.14.q_ref.k_ref.v_ref, f32[384,4096]{1,0:T(8,128)} %fusion.14.q_ref.k_ref.v_ref, f32[8,2,128]{2,1,0:T(2,128)} %bitcast.364, f32[8,1,128]{2,1,0:T(1,128)} %reshape_reshape.13.kn_ref, ...), custom_call_target="tpu_custom_call" | custom-call | flops 1500000000 | bytes 12000000 | tf_op jit(solution)/shard_map/attn_fwd/pallas_call | solution.py:131
  269.0 43.9 %all-gather.11.cloned.1.call-done = bf16[1024,10240]{1,0:T(8,128)(2,1)} async-done(((bf16[64,10240]{1,0:T(8,128)(2,1)}), bf16[1024,10240]{1,0:T(8,128)(2,1)}) %all-gather.11.cloned.1.call-update) | async-done | bytes 20971536 | tf_op jit(solution)/shard_map/all_gather | solution.py:255
  313.0 9.7 fusion.10.q_ref.k_ref.v_ref
  322.6 19.5 %attn_fwd.3 = bf16[384,2048]{1,0:T(8,128)(2,1)} custom-call(f32[384,4096]{1,0:T(8,128)} %fusion.10.q_ref.k_ref.v_ref, f32[384,4096]{1,0:T(8,128)} %fusion.10.q_ref.k_ref.v_ref, f32[384,4096]{1,0:T(8,128)} %fusion.10.q_ref.k_ref.v_ref, f32[8,2,128]{2,1,0:T(2,128)} %bitcast.366, f32[8,1,128]{2,1,0:T(1,128)} %reshape_reshape.15.kn_ref, ...), custom_call_target="tpu_custom_call" | custom-call | flops 1500000000 | bytes 12000000 | tf_op jit(solution)/shard_map/attn_fwd/pallas_call | solution.py:131
  342.2 31.2 %attn_bwd.2 = (bf16[384,4096]{1,0:T(8,128)(2,1)}, f32[8,2,128]{2,1,0:T(2,128)}, f32[8,1,128]{2,1,0:T(1,128)}) custom-call(f32[384,4096]{1,0:T(8,128)} %fusion.10.q_ref.k_ref.v_ref, f32[384,4096]{1,0:T(8,128)} %fusion.10.q_ref.k_ref.v_ref, f32[384,4096]{1,0:T(8,128)} %fusion.10.q_ref.k_ref.v_ref, bf16[384,2048]{1,0:T(8,128)(2,1)} %fusion.65.do_ref, ...), custom_call_target="tpu_custom_call" | custom-call | flops 4000000000 | bytes 15000000 | tf_op jit(solution)/shard_map/attn_bwd/pallas_call | solution.py:145
  381.6 10.6 fusion.18
  392.3 12.4 fusion
  404.7 8.3 fusion.129
  415.3 12.3 fusion.21
  451.0 31.4 %attn_bwd.3 = (bf16[384,4096]{1,0:T(8,128)(2,1)}, f32[8,2,128]{2,1,0:T(2,128)}, f32[8,1,128]{2,1,0:T(1,128)}) custom-call(f32[384,4096]{1,0:T(8,128)} %fusion.14.q_ref.k_ref.v_ref, f32[384,4096]{1,0:T(8,128)} %fusion.14.q_ref.k_ref.v_ref, f32[384,4096]{1,0:T(8,128)} %fusion.14.q_ref.k_ref.v_ref, bf16[384,2048]{1,0:T(8,128)(2,1)} %convolution_convert_fusion.do_ref, ...), custom_call_target="tpu_custom_call" | custom-call | flops 4000000000 | bytes 15000000 | tf_op jit(solution)/shard_map/attn_bwd/pallas_call | solution.py:145
  487.6 11.1 fusion.4
  592.8 27.5 %collective-permute-done.14 = f32[512,1024]{1,0:T(8,128)S(1)} collective-permute-done((f32[512,1024]{1,0:T(8,128)S(1)}, f32[512,1024]{1,0:T(8,128)S(1)}, u32[]{:S(2)}, u32[]{:S(2)}) %collective-permute-start.14) | collective-permute-done | bytes 2097184 | tf_op jit(solution)/shard_map/ppermute | solution.py:198
  621.0 43.4 %collective-permute-done.38 = f32[512,1024]{1,0:T(8,128)S(1)} collective-permute-done((f32[512,1024]{1,0:T(8,128)S(1)}, f32[512,1024]{1,0:T(8,128)S(1)}, u32[]{:S(2)}, u32[]{:S(2)}) %collective-permute-start.38) | collective-permute-done | bytes 2097184 | tf_op jit(solution)/shard_map/ppermute | solution.py:198
  677.8 146.0 %collective-permute-done.15 = f32[256,1024]{1,0:T(8,128)S(1)} collective-permute-done((f32[256,1024]{1,0:T(8,128)S(1)}, f32[256,1024]{1,0:T(8,128)S(1)}, u32[]{:S(2)}, u32[]{:S(2)}) %collective-permute-start.15) | collective-permute-done | bytes 1048608 | tf_op jit(solution)/shard_map/ppermute | solution.py:198
  834.0 13.5 collective-permute-done.39
  868.1 8.5 collective-permute-done.40
  909.6 12.1 collective-permute-done.9
  925.4 41.3 %collective-permute-done.33 = f32[256,2048]{1,0:T(8,128)} collective-permute-done((f32[256,2048]{1,0:T(8,128)}, f32[256,2048]{1,0:T(8,128)}, u32[]{:S(2)}, u32[]{:S(2)}) %collective-permute-start.33) | collective-permute-done | bytes 2097184 | tf_op jit(solution)/shard_map/ppermute | solution.py:198
  974.6 25.8 %collective-permute-done.26 = f32[384,1024]{1,0:T(8,128)} collective-permute-done((f32[384,1024]{1,0:T(8,128)}, f32[384,1024]{1,0:T(8,128)}, u32[]{:S(2)}, u32[]{:S(2)}) %collective-permute-start.26) | collective-permute-done | bytes 1572896 | tf_op jit(solution)/shard_map/ppermute | solution.py:198
  1003.7 30.3 %collective-permute-done.50 = f32[384,1024]{1,0:T(8,128)S(1)} collective-permute-done((f32[384,1024]{1,0:T(8,128)S(1)}, f32[384,1024]{1,0:T(8,128)S(1)}, u32[]{:S(2)}, u32[]{:S(2)}) %collective-permute-start.50) | collective-permute-done | bytes 1572896 | tf_op jit(solution)/shard_map/ppermute | solution.py:198
  1038.4 85.4 %collective-permute-done.7 = f32[128,2048]{1,0:T(8,128)S(1)} collective-permute-done((f32[128,2048]{1,0:T(8,128)}, f32[128,2048]{1,0:T(8,128)S(1)}, u32[]{:S(2)}, u32[]{:S(2)}) %collective-permute-start.7) | collective-permute-done | bytes 1048608 | tf_op jit(solution)/shard_map/ppermute | solution.py:198
  1131.1 11.5 collective-permute-done.31
  1152.8 73.0 %collective-permute-done.51 = f32[192,1024]{1,0:T(8,128)} collective-permute-done((f32[192,1024]{1,0:T(8,128)S(1)}, f32[192,1024]{1,0:T(8,128)}, u32[]{:S(2)}, u32[]{:S(2)}) %collective-permute-start.51) | collective-permute-done | bytes 786464 | tf_op jit(solution)/shard_map/ppermute | solution.py:198
  1240.8 64.5 %collective-permute-done.8 = f32[64,2048]{1,0:T(8,128)S(1)} collective-permute-done((f32[64,2048]{1,0:T(8,128)S(1)}, f32[64,2048]{1,0:T(8,128)S(1)}, u32[]{:S(2)}, u32[]{:S(2)}) %collective-permute-start.8) | collective-permute-done | bytes 524320 | tf_op jit(solution)/shard_map/ppermute | solution.py:198
  1325.6 28.4 %collective-permute-done.19 = f32[128,3072]{1,0:T(8,128)S(1)} collective-permute-done((f32[128,3072]{1,0:T(8,128)}, f32[128,3072]{1,0:T(8,128)S(1)}, u32[]{:S(2)}, u32[]{:S(2)}) %collective-permute-start.19) | collective-permute-done | bytes 1572896 | tf_op jit(solution)/shard_map/ppermute | solution.py:198
  1357.7 20.1 %collective-permute-done.43 = f32[128,3072]{1,0:T(8,128)S(1)} collective-permute-done((f32[128,3072]{1,0:T(8,128)}, f32[128,3072]{1,0:T(8,128)S(1)}, u32[]{:S(2)}, u32[]{:S(2)}) %collective-permute-start.43) | collective-permute-done | bytes 1572896 | tf_op jit(solution)/shard_map/ppermute | solution.py:198
  1382.7 11.1 collective-permute-done.20
  (552 shorter events, 369.1 us)
Async XLA Ops:
  7.2 62.4 %all-gather.9.cloned.1.call-start = ((), (), s32[]{:S(2)}) async-start(), calls=%async_computation.1 | async-start | bytes 11141120 | tf_op jit(solution)/shard_map/all_gather | solution.py:255
  9.3 119.0 %all-gather.13.cloned.1.call-start = ((), (), s32[]{:S(2)}) async-start(), calls=%async_computation.3 | async-start | bytes 11141120 | tf_op jit(solution)/shard_map/all_gather | solution.py:255
  11.4 209.3 %all-gather.7.cloned.1.call-start = ((), (), s32[]{:S(2)}) async-start(), calls=%async_computation | async-start | bytes 22282240 | tf_op jit(solution)/shard_map/all_gather | solution.py:255
  12.8 300.1 %all-gather.11.cloned.1.call-start = ((), (), s32[]{:S(2)}) async-start(), calls=%async_computation.2 | async-start | bytes 22282240 | tf_op jit(solution)/shard_map/all_gather | solution.py:255
  431.9 131.8 %collective-permute-start.13 = (bf16[384,1024]{1,0:T(8,128)(2,1)}, bf16[384,1024]{1,0:T(8,128)(2,1)}, u32[]{:S(2)}, u32[]{:S(2)}) collective-permute-start(bf16[384,1024]{1,0:T(8,128)(2,1)} %add_convert_fusion.1), channel_id=1, source_target_pairs={{0,1},{1,0},{2,3},{3,2},{4,5},{5,4},{6,7},{7,6},{8,9},{9,8},{10,11... | collective-permute-start | bytes 2359304 | tf_op jit(solution)/shard_map/ppermute | solution.py:169
  482.4 186.2 %collective-permute-start.5 = (bf16[384,4096]{1,0:T(8,128)(2,1)}, bf16[384,4096]{1,0:T(8,128)(2,1)}, u32[]{:S(2)}, u32[]{:S(2)}) collective-permute-start(bf16[384,4096]{1,0:T(8,128)(2,1)} %get-tuple-element.46), channel_id=1, source_target_pairs={{0,1},{1,0},{2,3},{3,2},{4,5},{5,4},{6,7},{7,6},{8,9},{9,8},{10,11... | collective-permute-start | bytes 9437192 | tf_op jit(solution)/shard_map/ppermute | solution.py:169
  563.1 106.7 %collective-permute-start.29 = (bf16[384,4096]{1,0:T(8,128)(2,1)}, bf16[384,4096]{1,0:T(8,128)(2,1)S(1)}, u32[]{:S(2)}, u32[]{:S(2)}) collective-permute-start(bf16[384,4096]{1,0:T(8,128)(2,1)} %get-tuple-element.52), channel_id=1, source_target_pairs={{0,1},{1,0},{2,3},{3,2},{4,5},{5,4},{6,7},{7,6},{8,9},{9,8},{10,11... | collective-permute-start | bytes 9437192 | tf_op jit(solution)/shard_map/ppermute | solution.py:169
  575.6 88.9 %collective-permute-start.38 = (f32[512,1024]{1,0:T(8,128)S(1)}, f32[512,1024]{1,0:T(8,128)S(1)}, u32[]{:S(2)}, u32[]{:S(2)}) collective-permute-start(f32[512,1024]{1,0:T(8,128)S(1)} %fusion.176), channel_id=1, source_target_pairs={{0,8},{8,0},{1,9},{9,1},{2,10},{10,2},{3,11},{11,3},{4,12},{12,4},... | collective-permute-start | bytes 6291464 | tf_op jit(solution)/shard_map/ppermute | solution.py:198
  583.1 297.1 %collective-permute-start.17 = (bf16[384,6144]{1,0:T(8,128)(2,1)S(1)}, bf16[384,6144]{1,0:T(8,128)(2,1)S(1)}, u32[]{:S(2)}, u32[]{:S(2)}) collective-permute-start(bf16[384,6144]{1,0:T(8,128)(2,1)S(1)} %bitcast.345), channel_id=1, source_target_pairs={{0,1},{1,0},{2,3},{3,2},{4,5},{5,4},{6,7},{7,6},{8,9},{9,8},{10,11... | collective-permute-start | bytes 14155784 | tf_op jit(solution)/shard_map/ppermute | solution.py:169
  620.3 263.1 %collective-permute-start.41 = (bf16[384,6144]{1,0:T(8,128)(2,1)S(1)}, bf16[384,6144]{1,0:T(8,128)(2,1)}, u32[]{:S(2)}, u32[]{:S(2)}) collective-permute-start(bf16[384,6144]{1,0:T(8,128)(2,1)S(1)} %bitcast.343), channel_id=1, source_target_pairs={{0,1},{1,0},{2,3},{3,2},{4,5},{5,4},{6,7},{7,6},{8,9},{9,8},{10,11... | collective-permute-start | bytes 14155784 | tf_op jit(solution)/shard_map/ppermute | solution.py:169
  664.4 186.1 %collective-permute-start.25 = (f32[768,1024]{1,0:T(8,128)}, f32[768,1024]{1,0:T(8,128)}, u32[]{:S(2)}, u32[]{:S(2)}) collective-permute-start(f32[768,1024]{1,0:T(8,128)} %fusion.151), channel_id=1, source_target_pairs={{0,2},{2,0},{1,3},{3,1},{4,6},{6,4},{5,7},{7,5},{8,10},{10,8},{9,1... | collective-permute-start | bytes 9437192 | tf_op jit(solution)/shard_map/ppermute | solution.py:198
  668.6 186.1 %collective-permute-start.49 = (f32[768,1024]{1,0:T(8,128)}, f32[768,1024]{1,0:T(8,128)}, u32[]{:S(2)}, u32[]{:S(2)}) collective-permute-start(f32[768,1024]{1,0:T(8,128)} %fusion.159), channel_id=1, source_target_pairs={{0,2},{2,0},{1,3},{3,1},{4,6},{6,4},{5,7},{7,5},{8,10},{10,8},{9,1... | collective-permute-start | bytes 9437192 | tf_op jit(solution)/shard_map/ppermute | solution.py:198
  671.4 152.4 %collective-permute-start.15 = (f32[256,1024]{1,0:T(8,128)S(1)}, f32[256,1024]{1,0:T(8,128)S(1)}, u32[]{:S(2)}, u32[]{:S(2)}) collective-permute-start(f32[256,1024]{1,0:T(8,128)S(1)} %convolution_add_fusion.21), channel_id=1, source_target_pairs={{0,2},{2,0},{1,3},{3,1},{4,6},{6,4},{5,7},{7,5},{8,10},{10,8},{9,1... | collective-permute-start | bytes 3145736 | tf_op jit(solution)/shard_map/ppermute | solution.py:198
  847.5 58.4 %collective-permute-start.6 = (f32[256,2048]{1,0:T(8,128)}, f32[256,2048]{1,0:T(8,128)}, u32[]{:S(2)}, u32[]{:S(2)}) collective-permute-start(f32[256,2048]{1,0:T(8,128)} %fusion.104), channel_id=1, source_target_pairs={{0,2},{2,0},{1,3},{3,1},{4,6},{6,4},{5,7},{7,5},{8,10},{10,8},{9,1... | collective-permute-start | bytes 6291464 | tf_op jit(solution)/shard_map/ppermute | solution.py:198
  865.4 56.3 %collective-permute-start.9 = (f32[256,2048]{1,0:T(8,128)}, f32[256,2048]{1,0:T(8,128)}, u32[]{:S(2)}, u32[]{:S(2)}) collective-permute-start(f32[256,2048]{1,0:T(8,128)} %fusion.98), channel_id=1, source_target_pairs={{0,4},{4,0},{1,5},{5,1},{2,6},{6,2},{3,7},{7,3},{8,12},{12,8},{9,1... | collective-permute-start | bytes 6291464 | tf_op jit(solution)/shard_map/ppermute | solution.py:198
  876.6 93.4 %collective-permute-start.30 = (f32[256,2048]{1,0:T(8,128)}, f32[256,2048]{1,0:T(8,128)}, u32[]{:S(2)}, u32[]{:S(2)}) collective-permute-start(f32[256,2048]{1,0:T(8,128)} %fusion.90), channel_id=1, source_target_pairs={{0,2},{2,0},{1,3},{3,1},{4,6},{6,4},{5,7},{7,5},{8,10},{10,8},{9,1... | collective-permute-start | bytes 6291464 | tf_op jit(solution)/shard_map/ppermute | solution.py:198
  882.4 84.3 %collective-permute-start.33 = (f32[256,2048]{1,0:T(8,128)}, f32[256,2048]{1,0:T(8,128)}, u32[]{:S(2)}, u32[]{:S(2)}) collective-permute-start(f32[256,2048]{1,0:T(8,128)} %fusion.84), channel_id=1, source_target_pairs={{0,4},{4,0},{1,5},{5,1},{2,6},{6,2},{3,7},{7,3},{8,12},{12,8},{9,1... | collective-permute-start | bytes 6291464 | tf_op jit(solution)/shard_map/ppermute | solution.py:198
  883.5 116.9 %collective-permute-start.26 = (f32[384,1024]{1,0:T(8,128)}, f32[384,1024]{1,0:T(8,128)}, u32[]{:S(2)}, u32[]{:S(2)}) collective-permute-start(f32[384,1024]{1,0:T(8,128)} %slice_add_fusion.1), channel_id=1, source_target_pairs={{0,4},{4,0},{1,5},{5,1},{2,6},{6,2},{3,7},{7,3},{8,12},{12,8},{9,1... | collective-permute-start | bytes 4718600 | tf_op jit(solution)/shard_map/ppermute | solution.py:198
  906.0 128.0 %collective-permute-start.50 = (f32[384,1024]{1,0:T(8,128)S(1)}, f32[384,1024]{1,0:T(8,128)S(1)}, u32[]{:S(2)}, u32[]{:S(2)}) collective-permute-start(f32[384,1024]{1,0:T(8,128)S(1)} %copy-done.51), channel_id=1, source_target_pairs={{0,4},{4,0},{1,5},{5,1},{2,6},{6,2},{3,7},{7,3},{8,12},{12,8},{9,1... | collective-permute-start | bytes 4718600 | tf_op jit(solution)/shard_map/ppermute | solution.py:198
  921.7 387.6 %collective-permute-start.18 = (f32[256,3072]{1,0:T(8,128)}, f32[256,3072]{1,0:T(8,128)S(1)}, u32[]{:S(2)}, u32[]{:S(2)}) collective-permute-start(f32[256,3072]{1,0:T(8,128)} %fusion.62), channel_id=1, source_target_pairs={{0,4},{4,0},{1,5},{5,1},{2,6},{6,2},{3,7},{7,3},{8,12},{12,8},{9,1... | collective-permute-start | bytes 9437192 | tf_op jit(solution)/shard_map/ppermute | solution.py:198
  966.6 157.2 %collective-permute-start.7 = (f32[128,2048]{1,0:T(8,128)}, f32[128,2048]{1,0:T(8,128)S(1)}, u32[]{:S(2)}, u32[]{:S(2)}) collective-permute-start(f32[128,2048]{1,0:T(8,128)} %fusion.107), channel_id=1, source_target_pairs={{0,4},{4,0},{1,5},{5,1},{2,6},{6,2},{3,7},{7,3},{8,12},{12,8},{9,1... | collective-permute-start | bytes 3145736 | tf_op jit(solution)/shard_map/ppermute | solution.py:198
  970.1 157.8 %collective-permute-start.10 = (f32[128,2048]{1,0:T(8,128)}, f32[128,2048]{1,0:T(8,128)}, u32[]{:S(2)}, u32[]{:S(2)}) collective-permute-start(f32[128,2048]{1,0:T(8,128)} %convolution_add_fusion.11), channel_id=1, source_target_pairs={{0,8},{8,0},{1,9},{9,1},{2,10},{10,2},{3,11},{11,3},{4,12},{12,4},... | collective-permute-start | bytes 3145736 | tf_op jit(solution)/shard_map/ppermute | solution.py:198
  1000.3 142.3 %collective-permute-start.31 = (f32[128,2048]{1,0:T(8,128)}, f32[128,2048]{1,0:T(8,128)S(1)}, u32[]{:S(2)}, u32[]{:S(2)}) collective-permute-start(f32[128,2048]{1,0:T(8,128)} %fusion.93), channel_id=1, source_target_pairs={{0,4},{4,0},{1,5},{5,1},{2,6},{6,2},{3,7},{7,3},{8,12},{12,8},{9,1... | collective-permute-start | bytes 3145736 | tf_op jit(solution)/shard_map/ppermute | solution.py:198
  1033.9 112.7 %collective-permute-start.34 = (f32[128,2048]{1,0:T(8,128)}, f32[128,2048]{1,0:T(8,128)}, u32[]{:S(2)}, u32[]{:S(2)}) collective-permute-start(f32[128,2048]{1,0:T(8,128)} %convolution_add_fusion.10), channel_id=1, source_target_pairs={{0,8},{8,0},{1,9},{9,1},{2,10},{10,2},{3,11},{11,3},{4,12},{12,4},... | collective-permute-start | bytes 3145736 | tf_op jit(solution)/shard_map/ppermute | solution.py:198
  1127.8 184.0 %collective-permute-start.21 = (f32[256,3072]{1,0:T(8,128)}, f32[256,3072]{1,0:T(8,128)S(1)}, u32[]{:S(2)}, u32[]{:S(2)}) collective-permute-start(f32[256,3072]{1,0:T(8,128)} %fusion.54), channel_id=1, source_target_pairs={{0,8},{8,0},{1,9},{9,1},{2,10},{10,2},{3,11},{11,3},{4,12},{12,4},... | collective-permute-start | bytes 9437192 | tf_op jit(solution)/shard_map/ppermute | solution.py:198
  1142.6 83.2 %collective-permute-start.51 = (f32[192,1024]{1,0:T(8,128)S(1)}, f32[192,1024]{1,0:T(8,128)}, u32[]{:S(2)}, u32[]{:S(2)}) collective-permute-start(f32[192,1024]{1,0:T(8,128)S(1)} %copy-done.67), channel_id=1, source_target_pairs={{0,8},{8,0},{1,9},{9,1},{2,10},{10,2},{3,11},{11,3},{4,12},{12,4},... | collective-permute-start | bytes 2359304 | tf_op jit(solution)/shard_map/ppermute | solution.py:198
  1146.6 168.2 %collective-permute-start.42 = (f32[256,3072]{1,0:T(8,128)}, f32[256,3072]{1,0:T(8,128)}, u32[]{:S(2)}, u32[]{:S(2)}) collective-permute-start(f32[256,3072]{1,0:T(8,128)} %fusion.48), channel_id=1, source_target_pairs={{0,4},{4,0},{1,5},{5,1},{2,6},{6,2},{3,7},{7,3},{8,12},{12,8},{9,1... | collective-permute-start | bytes 9437192 | tf_op jit(solution)/shard_map/ppermute | solution.py:198
  1147.2 80.1 %collective-permute-start.11 = (f32[64,2048]{1,0:T(8,128)}, f32[64,2048]{1,0:T(8,128)S(1)}, u32[]{:S(2)}, u32[]{:S(2)}) collective-permute-start(f32[64,2048]{1,0:T(8,128)} %fusion.75), channel_id=1, source_target_pairs={{0,2},{2,0},{1,3},{3,1},{4,6},{6,4},{5,7},{7,5},{8,10},{10,8},{9,1... | collective-permute-start | bytes 1572872 | tf_op jit(solution)/shard_map/ppermute | solution.py:198
  1225.8 93.6 %collective-permute-start.45 = (f32[256,3072]{1,0:T(8,128)}, f32[256,3072]{1,0:T(8,128)S(1)}, u32[]{:S(2)}, u32[]{:S(2)}) collective-permute-start(f32[256,3072]{1,0:T(8,128)} %fusion.40), channel_id=1, source_target_pairs={{0,8},{8,0},{1,9},{9,1},{2,10},{10,2},{3,11},{11,3},{4,12},{12,4},... | collective-permute-start | bytes 9437192 | tf_op jit(solution)/shard_map/ppermute | solution.py:198
  1236.6 68.7 %collective-permute-start.8 = (f32[64,2048]{1,0:T(8,128)S(1)}, f32[64,2048]{1,0:T(8,128)S(1)}, u32[]{:S(2)}, u32[]{:S(2)}) collective-permute-start(f32[64,2048]{1,0:T(8,128)S(1)} %copy-done.76), channel_id=1, source_target_pairs={{0,8},{8,0},{1,9},{9,1},{2,10},{10,2},{3,11},{11,3},{4,12},{12,4},... | collective-permute-start | bytes 1572872 | tf_op jit(solution)/shard_map/ppermute | solution.py:198
  1318.2 59.6 %collective-permute-start.43 = (f32[128,3072]{1,0:T(8,128)}, f32[128,3072]{1,0:T(8,128)S(1)}, u32[]{:S(2)}, u32[]{:S(2)}) collective-permute-start(f32[128,3072]{1,0:T(8,128)} %convolution_add_fusion), channel_id=1, source_target_pairs={{0,8},{8,0},{1,9},{9,1},{2,10},{10,2},{3,11},{11,3},{4,12},{12,4},... | collective-permute-start | bytes 4718600 | tf_op jit(solution)/shard_map/ppermute | solution.py:198
  1321.5 59.7 %collective-permute-start.46 = (f32[128,3072]{1,0:T(8,128)}, f32[128,3072]{1,0:T(8,128)S(1)}, u32[]{:S(2)}, u32[]{:S(2)}) collective-permute-start(f32[128,3072]{1,0:T(8,128)} %fusion.43), channel_id=1, source_target_pairs={{0,2},{2,0},{1,3},{3,1},{4,6},{6,4},{5,7},{7,5},{8,10},{10,8},{9,1... | collective-permute-start | bytes 4718600 | tf_op jit(solution)/shard_map/ppermute | solution.py:198
  (159 other events, 3409.9 us)
Sparse Core Ops, SparseCore 0:
  10.8 58.7 all-gather.8
  72.4 55.8 all-gather.12
  130.6 90.0 all-gather.6
  222.8 90.0 all-gather.10

commit v2 on v1

--- a/solution.py
+++ b/solution.py
@@ -169,24 +169,36 @@
     return lax.ppermute(value, 'c', SWAP)
 
 
-def pair_rows(act, block_rows, chip_pos, core):
-    act_t = act.T
-    tokens = act_t.shape[1]
-
-    def pick(which):
-        parts = []
-        for delta in range(8):
-            chip = 0
-            for axis in CHIP_AXES:
-                chip = chip + BIT[axis] * (chip_pos[axis] ^ (1 if delta & BIT[axis] else 0))
-            start = (chip * 2 + which) * block_rows
-            parts.append(lax.dynamic_slice(act_t, (start, 0), (block_rows, tokens)))
-        return jnp.concatenate(parts, axis=0)
-
-    mine = pick(core)
-    theirs = swap_cores(pick(1 - core))
-    both = jnp.concatenate([mine, theirs], axis=1)
-    return [both[d * block_rows:(d + 1) * block_rows] for d in range(8)]
+def pair_rows_kernel(index_ref, act_ref, mine_ref, theirs_ref, flip_ref):
+    rows = mine_ref.shape[0]
+    core = index_ref[8]
+    flip_ref[...] = act_ref[...].T
+    mine_ref[...] = flip_ref[pl.ds(pl.multiple_of(core * rows, rows), rows), :]
+    theirs_ref[...] = flip_ref[pl.ds(pl.multiple_of((1 - core) * rows, rows), rows), :]
+
+
+def pair_rows(act, dims, chip_pos, core):
+    tokens = act.shape[0]
+    rows = act.shape[1] // 16
+    deltas = [sum(BIT[dims[i]] * ((d >> (2 - i)) & 1) for i in range(3)) for d in range(8)]
+    chip = sum(BIT[axis] * chip_pos[axis] for axis in CHIP_AXES)
+    index = jnp.stack([chip ^ delta for delta in deltas] + [core]).astype(jnp.int32)
+    out_spec = pl.BlockSpec((rows, tokens), lambda d, idx: (d, 0))
+    mine, theirs = pl.pallas_call(
+        pair_rows_kernel,
+        grid_spec=pltpu.PrefetchScalarGridSpec(
+            num_scalar_prefetch=1,
+            grid=(8,),
+            in_specs=[pl.BlockSpec((tokens, 2 * rows), lambda d, idx: (0, idx[d]))],
+            out_specs=[out_spec, out_spec],
+            scratch_shapes=[pltpu.VMEM((2 * rows, tokens), BF16)],
+        ),
+        out_shape=[jax.ShapeDtypeStruct((8 * rows, tokens), BF16)] * 2,
+        cost_estimate=pl.CostEstimate(flops=300_000_000, bytes_accessed=4 * act.size, transcendentals=0),
+        name='pair_rows',
+    )(index, act)
+    both = jnp.concatenate([mine, swap_cores(theirs)], axis=1)
+    return {delta: both[d * rows:(d + 1) * rows] for d, delta in enumerate(deltas)}
 
 
 def pair_tokens(cot):
@@ -198,15 +210,18 @@
     return lax.ppermute(value, axis, SWAP)
 
 
-def reduce_group(blocks, cot, dims):
-    rows = blocks[0].shape[0]
+def reduce_group(blocks, cot, tag, sends):
+    rows, dims = blocks[0].shape[0], RING[tag]
 
     def part(b1, b2, b3):
         return blocks[b1 * BIT[dims[0]] + b2 * BIT[dims[1]] + b3 * BIT[dims[2]]]
 
-    send1 = dot32(jnp.concatenate([part(1, 0, 0), part(1, 0, 1), part(1, 1, 0), part(1, 1, 1)], axis=0), cot)
+    half = jnp.concatenate([part(1, 0, 0), part(1, 0, 1), part(1, 1, 0), part(1, 1, 1)], axis=0)
+    quarter = jnp.concatenate([part(0, 1, 0), part(0, 1, 1)], axis=0)
+    send1 = dot32(half, cot)
+    sends[tag] = send1
     got1 = hop(send1, dims[0])
-    send2 = dot32(jnp.concatenate([part(0, 1, 0), part(0, 1, 1)], axis=0), cot) + got1[2 * rows:]
+    send2 = dot32(quarter, cot) + got1[2 * rows:]
     got2 = hop(send2, dims[1])
     send3 = dot32(part(0, 0, 1), cot) + got1[rows:2 * rows] + got2[rows:]
     got3 = hop(send3, dims[2])
@@ -214,22 +229,29 @@
 
 
 def scatter_small(values, chip_pos, core):
-    value = values.reshape((2, 2, 2, 2) + values.shape[1:])
-    for axis, pos in (('c', core), ('x', chip_pos['x']), ('y', chip_pos['y']), ('z', chip_pos['z'])):
-        dim = {'z': 0, 'y': 1, 'x': 2, 'c': 3}[axis]
-        keep = lax.dynamic_index_in_dim(value, pos, dim, keepdims=False)
-        send = lax.dynamic_index_in_dim(value, 1 - pos, dim, keepdims=False)
-        value = keep + lax.ppermute(send, axis, SWAP)
-    return value
+    value = values.reshape(8, 2, -1)
+    keep = lax.dynamic_index_in_dim(value, core, 1, keepdims=False)
+    value = keep + hop(lax.dynamic_index_in_dim(value, 1 - core, 1, keepdims=False), 'c')
+    chip = sum(BIT[axis] * chip_pos[axis] for axis in CHIP_AXES)
+    total = lax.dynamic_index_in_dim(value, chip, 0, keepdims=False)
+    sends = [lax.dynamic_index_in_dim(value, chip ^ delta, 0, keepdims=False) for delta in range(1, 8)]
+    gots = [lax.ppermute(send, CHIP_AXES, [(i, i ^ delta) for i in range(8)]) for delta, send in enumerate(sends, 1)]
+    return sum(gots, total)
 
 
 RING = {
-    'o': ('z', 'x', 'y'),
-    'down': ('x', 'y', 'z'),
-    'gate': ('y', 'z', 'x'),
-    'up': ('z', 'x', 'y'),
-    'q': ('x', 'y', 'z'),
-    'kv': ('y', 'z', 'x'),
+    'down_0': ('x', 'y', 'z'),
+    'down_1': ('x', 'y', 'z'),
+    'gate_0': ('y', 'z', 'x'),
+    'gate_1': ('y', 'z', 'x'),
+    'kv_0': ('y', 'z', 'x'),
+    'kv_1': ('y', 'z', 'x'),
+    'o_0': ('z', 'x', 'y'),
+    'o_1': ('z', 'x', 'y'),
+    'q_0': ('x', 'y', 'z'),
+    'q_1': ('x', 'y', 'z'),
+    'up_0': ('z', 'x', 'y'),
+    'up_1': ('z', 'x', 'y'),
 }
 
 
@@ -257,14 +279,22 @@
         cos_full, sin_full = rope_tables(positions)
 
         weights = []
-        for _, w_q, w_k, w_v, w_o, w_gate, w_up, w_down, _, _ in layer_shards:
-            w_in = gather(jnp.concatenate([w_q, w_k, w_v, w_gate, w_up], axis=1))
+        for layer, (_, w_q, w_k, w_v, w_o, w_gate, w_up, w_down, _, _) in enumerate(layer_shards):
+            in_cols = jnp.concatenate([w_q, w_k, w_v, w_gate, w_up], axis=1)
             qkv_width = w_q.shape[1] + w_k.shape[1] + w_v.shape[1]
+            in_width = in_cols.shape[1]
+            rows_in, rows_o, rows_d = w_q.shape[0], w_o.shape[0], w_down.shape[0]
+            if layer == 0:
+                stacked = [m[i * rows_in:(i + 1) * rows_in] for m in (w_o, w_down) for i in range(m.shape[0] // rows_in)]
+                w_all = gather(jnp.concatenate([in_cols] + stacked, axis=1))
+                w_in = w_all[:, :in_width]
+                width = w_o.shape[1]
+                w_od = jnp.concatenate([w_all[:, in_width + i * width:in_width + (i + 1) * width].reshape(16, rows_in, width) for i in range(len(stacked))], axis=1)
+            else:
+                w_in = gather(in_cols)
+                w_od = gather(jnp.concatenate([w_o, w_down], axis=0)).reshape(16, rows_o + rows_d, -1)
             w_qkv, w_gu = w_in[:, :qkv_width], w_in[:, qkv_width:]
-            w_od = gather(jnp.concatenate([w_o, w_down], axis=0))
-            rows_o, rows_d = w_o.shape[0], w_down.shape[0]
-            w_od = w_od.reshape(16, rows_o + rows_d, -1)
-            weights.append((w_qkv, w_gu, w_od[:, :rows_o].reshape(16 * rows_o, -1), w_od[:, rows_o:].reshape(16 * rows_d, -1)))
+            weights.append((w_qkv, w_gu, w_od))
         vecs = jnp.concatenate([v for s in layer_shards for v in (s[0], s[8], s[9])])
         vec_sizes = [v.shape[0] for s in layer_shards for v in (s[0], s[8], s[9])]
         vecs = lax.all_gather(vecs, AX, axis=0, tiled=False)
@@ -273,10 +303,17 @@
             small.append(vecs[:, offset:offset + size].reshape(-1))
             offset += size
 
+        def split_od(w_od):
+            return w_od[:, :rows_o].reshape(16 * rows_o, -1), w_od[:, rows_o:].reshape(16 * rows_d, -1)
+
+        def layer_out(x_f32, attn_out, hidden, w_o_full, w_down_full):
+            layer_sum = x_f32 + dot32(attn_out, w_o_full) + dot32(hidden, w_down_full)
+            return layer_sum.astype(BF16)
+
         stream = x_in[0]
         saved = []
         for layer in range(2):
-            w_qkv, w_gu, w_o_full, w_down_full = weights[layer]
+            w_qkv, w_gu, w_od = weights[layer]
             ln_gamma = small[3 * layer]
             n_kv = small[3 * layer + 2].shape[0] // HEAD_DIM
             q_norm = small[3 * layer + 1].reshape(n_kv, -1, HEAD_DIM)
@@ -291,34 +328,42 @@
             ffn = gate_up.shape[1] // 2
             hidden32, swiglu_vjp = jax.vjp(swiglu, gate_up[:, :ffn], gate_up[:, ffn:])
             hidden = hidden32.astype(BF16)
-            layer_sum = x_f32 + dot32(attn_out, w_o_full) + dot32(hidden, w_down_full)
-            stream = layer_sum.astype(BF16)
-            saved.append((norm_vjp, normed, qkv, q_norm, k_norm, attn_out, swiglu_vjp, hidden, q_width, kv_width))
+            if layer == 0:
+                od_pair = split_od(w_od)
+                stream = layer_out(x_f32, attn_out, hidden, *od_pair)
+            saved.append((x_f32, norm_vjp, normed, qkv, q_norm, k_norm, attn_out, swiglu_vjp, hidden, q_width, kv_width))
 
         grad = grad_out[0]
         out_grads = [None, None]
+        sends = {}
         small_grads = [None, None]
         for layer in (1, 0):
-            norm_vjp, normed, qkv, q_norm, k_norm, attn_out, swiglu_vjp, hidden, q_width, kv_width = saved[layer]
-            w_qkv, w_gu, w_o_full, w_down_full = weights[layer]
+            x_f32, norm_vjp, normed, qkv, q_norm, k_norm, attn_out, swiglu_vjp, hidden, q_width, kv_width = saved[layer]
+            w_qkv, w_gu, w_od = weights[layer]
             ffn = hidden.shape[1]
             grad2 = pair_tokens(grad)
-            attn_rows = pair_rows(attn_out, attn_out.shape[1] // 16, chip_pos, core)
-            g_o = reduce_group(attn_rows, grad2, RING['o'])
-            hidden_rows = pair_rows(hidden, ffn // 16, chip_pos, core)
-            g_down = reduce_group(hidden_rows, grad2, RING['down'])
+            attn_rows = pair_rows(attn_out, RING['o_' + str(layer)], chip_pos, core)
+            g_o = reduce_group(attn_rows, grad2, 'o_' + str(layer), sends)
+            hidden_rows = pair_rows(hidden, RING['down_' + str(layer)], chip_pos, core)
+            g_down = reduce_group(hidden_rows, grad2, 'down_' + str(layer), sends)
+            if layer == 1:
+                w_od, _ = lax.optimization_barrier((w_od, sends['down_1']))
+                w_o_full, w_down_full = split_od(w_od)
+                stream = layer_out(x_f32, attn_out, hidden, w_o_full, w_down_full)
+            else:
+                w_o_full, w_down_full = od_pair
             d_hidden = dot_t32(grad, w_down_full)
             d_gate, d_up = swiglu_vjp(d_hidden)
             d_gu = jnp.concatenate([d_gate.astype(BF16), d_up.astype(BF16)], axis=1)
-            normed_rows = pair_rows(normed, normed.shape[1] // 16, chip_pos, core)
+            normed_rows = pair_rows(normed, CHIP_AXES, chip_pos, core)
             d_gu2 = pair_tokens(d_gu)
-            g_gate = reduce_group(normed_rows, d_gu2[:, :ffn], RING['gate'])
-            g_up = reduce_group(normed_rows, d_gu2[:, ffn:], RING['up'])
+            g_gate = reduce_group(normed_rows, d_gu2[:, :ffn], 'gate_' + str(layer), sends)
+            g_up = reduce_group(normed_rows, d_gu2[:, ffn:], 'up_' + str(layer), sends)
             d_attn = dot_t32(grad, w_o_full).astype(BF16)
             d_qkv, g_q_norm, g_k_norm = attention_bwd(qkv, d_attn, q_norm, k_norm, cos_full, sin_full)
             d_qkv2 = pair_tokens(d_qkv)
-            g_q = reduce_group(normed_rows, d_qkv2[:, :q_width], RING['q'])
-            g_kv = reduce_group(normed_rows, d_qkv2[:, q_width:], RING['kv'])
+            g_q = reduce_group(normed_rows, d_qkv2[:, :q_width], 'q_' + str(layer), sends)
+            g_kv = reduce_group(normed_rows, d_qkv2[:, q_width:], 'kv_' + str(layer), sends)
             d_normed = dot_t32(d_gu, w_gu) + dot_t32(d_qkv, w_qkv)
             d_stream, g_ln = norm_vjp(d_normed)
             grad = (grad.astype(F32) + d_stream).astype(BF16)

time: 1420 us -> 1170 us (0.82)
  waiting for transfers between devices: 855 us -> 592 us
  Pallas kernels: 101 us -> 141 us
  local copies, waits for them, and re-layouts: 113 us -> 80.1 us
    ppermute x36 -> x37, waiting for transfers between devices: 656 us -> 430 us  [hop(): return lax.ppermute(value, axis, SWAP)]
    all_gather x4 -> x3, waiting for transfers between devices: 198 us -> 97.4 us  [gather(): return lax.all_gather(piece, AX, axis=0, tiled=True)]
    ppermute x4 -> x7, waiting for transfers between devices: 0.59 us -> 64.2 us  [scatter_small(): lax.ppermute(send, CHIP_AXES, [(i, i ^ delta) for i in range(8)])]
    pallas_call x0 -> x6, Pallas kernels: none -> 39.1 us  [pair_rows(): pl.pallas_call(pair_rows_kernel, grid_spec=pltpu.PrefetchScalarGridSpec(n...]
    concatenate x12 -> x8, local copies, waits for them, and re-layouts: 24.5 us -> 5.56 us  [the longest x6 4.45 us: pair_rows(): both = jnp.concatenate([mine, swap_cores(theirs)], axis=1)]
    unnamed x302 -> x239, local copies, waits for them, and re-layouts: 39.3 us -> 34.2 us
    ppermute x36 -> x37, starting transfers between devices: 34.4 us -> 36.9 us  [hop(): return lax.ppermute(value, axis, SWAP)]
  transfers between devices with their start and end apart: 56 -> 59, of which waited for: 27 -> 20; matrix products, arithmetic and copies ran while one was open for 22% -> 27% of each run, Pallas kernels for 4% -> 12%
where the time goes in v2:
time: 1170 us; the launch traced here: 1150 us
  waiting for transfers between devices  592 us (51%)
  matrix products  228 us (19%)
  Pallas kernels  141 us (12%)
  local copies, waits for them, and re-layouts  80.1 us (7%)
  starting transfers between devices  49.6 us (4%)
  other arithmetic  32.9 us (3%)
  between operations  16.2 us (1%)
  blocking collectives  15.1 us (1%)
    ppermute x37, waiting for transfers between devices, hop(): return lax.ppermute(value, axis, SWAP)  430 us
    dot_general x56, matrix products, dot32(): return jnp.dot(a, b, preferred_element_type=F32)  161 us
    all_gather x3, waiting for transfers between devices, gather(): return lax.all_gather(piece, AX, axis=0, tiled=True)  97.4 us
    dot_general x8, matrix products, dot_t32(): lax.dot_general(a, b, (((1,), (1,)), ((), ())), preferred_element_type=F32)  66.4 us
    ppermute x7, waiting for transfers between devices, scatter_small(): lax.ppermute(send, CHIP_AXES, [(i, i ^ delta) for i in range(8)])  64.2 us
    pallas_call x2, Pallas kernels, attention_bwd(): pl.pallas_call(attn_bwd_kernel, grid=(n_kv,), in_specs=[q_spec, k_spec, v...  62.8 us
    pallas_call x6, Pallas kernels, pair_rows(): pl.pallas_call(pair_rows_kernel, grid_spec=pltpu.PrefetchScalarGridSpec(n...  39.1 us
    pallas_call x2, Pallas kernels, attention_fwd(): pl.pallas_call(attn_fwd_kernel, grid=(n_kv,), in_specs=[q_spec, k_spec, v...  38.6 us
  transfers between devices with their start and end apart: 59, of which 20 were waited for; matrix products, arithmetic and copies ran while one was open for 27% of the time, Pallas kernels for 12%

profile of v2, /device:TPU:0, one launch (start us, length us, event | category | flops | bytes accessed | tf_op | source)
XLA Modules:
  0.0 1153.7 jit_solution(11649080092906055057)
XLA Ops:
  21.1 15.1 %all-gather.1 = f32[16,1,512]{2,1,0:T(1,128)S(1)} all-gather(f32[1,1,512]{2,1,0:T(1,128)S(1)} %bitcast.168), channel_id=2, replica_groups=mesh['z'=2,'y'=2,'x'=2,'c'=2] {'z','y','x','c'}, dimensions={0}, use_global_device_ids=true | all-gather | bytes 34816 | tf_op jit(solution)/shard_map/all_gather | solution.py:300
  54.8 86.3 %all-gather.6.cloned.1.call-done = bf16[1024,15360]{1,0:T(8,128)(2,1)} async-done(((bf16[64,15360]{1,0:T(8,128)(2,1)}), bf16[1024,15360]{1,0:T(8,128)(2,1)}) %all-gather.6.cloned.1.call-update) | async-done | bytes 31457296 | tf_op jit(solution)/shard_map/all_gather | solution.py:277
  141.1 10.0 fusion.14.q_ref.k_ref.v_ref
  151.1 19.4 %attn_fwd.2.act_ref = bf16[384,2048]{1,0:T(8,128)(2,1)} custom-call(f32[384,4096]{1,0:T(8,128)} %fusion.14.q_ref.k_ref.v_ref, f32[384,4096]{1,0:T(8,128)} %fusion.14.q_ref.k_ref.v_ref, f32[384,4096]{1,0:T(8,128)} %fusion.14.q_ref.k_ref.v_ref, f32[8,2,128]{2,1,0:T(2,128)} %bitcast.162, f32[8,1,128]{2,1,0:T(1,128)} %reshape_reshape.13.kn_ref, ...), custom_call_target="tpu_custom_call" | custom-call | flops 1500000000 | bytes 12000000 | tf_op jit(solution)/shard_map/attn_fwd/pallas_call | solution.py:131
  177.3 8.0 fusion.6
  191.2 7.1 pair_rows.9
  222.4 11.1 all-gather.8.cloned.1.call-done
  233.5 9.7 fusion.10.q_ref.k_ref.v_ref
  243.2 19.2 %attn_fwd.3.act_ref = bf16[384,2048]{1,0:T(8,128)(2,1)} custom-call(f32[384,4096]{1,0:T(8,128)} %fusion.10.q_ref.k_ref.v_ref, f32[384,4096]{1,0:T(8,128)} %fusion.10.q_ref.k_ref.v_ref, f32[384,4096]{1,0:T(8,128)} %fusion.10.q_ref.k_ref.v_ref, f32[8,2,128]{2,1,0:T(2,128)} %bitcast.164, f32[8,1,128]{2,1,0:T(1,128)} %reshape_reshape.15.kn_ref, ...), custom_call_target="tpu_custom_call" | custom-call | flops 1500000000 | bytes 12000000 | tf_op jit(solution)/shard_map/attn_fwd/pallas_call | solution.py:131
  269.2 9.1 fusion.2
  284.3 7.0 pair_rows.6
  322.0 10.5 fusion.18
  339.3 31.2 %attn_bwd.2 = (bf16[384,4096]{1,0:T(8,128)(2,1)}, f32[8,2,128]{2,1,0:T(2,128)}, f32[8,1,128]{2,1,0:T(1,128)}) custom-call(f32[384,4096]{1,0:T(8,128)} %fusion.10.q_ref.k_ref.v_ref, f32[384,4096]{1,0:T(8,128)} %fusion.10.q_ref.k_ref.v_ref, f32[384,4096]{1,0:T(8,128)} %fusion.10.q_ref.k_ref.v_ref, bf16[384,2048]{1,0:T(8,128)(2,1)} %fusion.57.do_ref, ...), custom_call_target="tpu_custom_call" | custom-call | flops 4000000000 | bytes 15000000 | tf_op jit(solution)/shard_map/attn_bwd/pallas_call | solution.py:145
  375.6 11.1 fusion
  386.6 7.3 fusion.113
  396.5 12.0 %fusion.21 = (bf16[384,3072]{1,0:T(8,128)(2,1)}, bf16[384,3072]{1,0:T(8,128)(2,1)}) fusion(f32[384,6144]{1,0:T(8,128)} %copy-done.3, bf16[384,1024]{1,0:T(8,128)(2,1)} %add_convert_fusion.1, bf16[3072,1024]{1,0:T(8,128)(2,1)} %bitcast.151), kind=kOutput, calls=%fused_computation.24 | convolution fusion | flops 2432434176 | bytes 21233664 | tf_op jit(solution)/shard_map/dot_general | solution.py:165
  415.6 31.6 %attn_bwd.3 = (bf16[384,4096]{1,0:T(8,128)(2,1)}, f32[8,2,128]{2,1,0:T(2,128)}, f32[8,1,128]{2,1,0:T(1,128)}) custom-call(f32[384,4096]{1,0:T(8,128)} %fusion.14.q_ref.k_ref.v_ref, f32[384,4096]{1,0:T(8,128)} %fusion.14.q_ref.k_ref.v_ref, f32[384,4096]{1,0:T(8,128)} %fusion.14.q_ref.k_ref.v_ref, bf16[384,2048]{1,0:T(8,128)(2,1)} %convolution_convert_fusion.do_ref, ...), custom_call_target="tpu_custom_call" | custom-call | flops 4000000000 | bytes 15000000 | tf_op jit(solution)/shard_map/attn_bwd/pallas_call | solution.py:145
  452.8 11.1 fusion.4
  463.9 7.2 fusion.109
  495.6 64.2 %collective-permute-done.5 = f32[512]{0:T(512)S(1)} collective-permute-done((f32[512]{0:T(512)S(1)}, f32[512]{0:T(512)S(1)}, u32[]{:S(2)}, u32[]{:S(2)}) %collective-permute-start.5) | collective-permute-done | bytes 2080 | tf_op jit(solution)/shard_map/ppermute | solution.py:238
  566.4 19.0 %collective-permute-done.44 = f32[256,1024]{1,0:T(8,128)S(1)} collective-permute-done((f32[256,1024]{1,0:T(8,128)S(1)}, f32[256,1024]{1,0:T(8,128)S(1)}, u32[]{:S(2)}, u32[]{:S(2)}) %collective-permute-start.44) | collective-permute-done | bytes 1048608 | tf_op jit(solution)/shard_map/ppermute | solution.py:210
  610.5 73.8 %collective-permute-done.21 = f32[256,1024]{1,0:T(8,128)} collective-permute-done((f32[256,1024]{1,0:T(8,128)}, f32[256,1024]{1,0:T(8,128)}, u32[]{:S(2)}, u32[]{:S(2)}) %collective-permute-start.21) | collective-permute-done | bytes 1048608 | tf_op jit(solution)/shard_map/ppermute | solution.py:210
  694.4 38.5 %collective-permute-done.22 = f32[128,1024]{1,0:T(8,128)S(1)} collective-permute-done((f32[128,1024]{1,0:T(8,128)S(1)}, f32[128,1024]{1,0:T(8,128)S(1)}, u32[]{:S(2)}, u32[]{:S(2)}) %collective-permute-start.22) | collective-permute-done | bytes 524320 | tf_op jit(solution)/shard_map/ppermute | solution.py:210
  766.5 11.5 collective-permute-done.15
  786.1 36.8 %collective-permute-done.39 = f32[256,2048]{1,0:T(8,128)} collective-permute-done((f32[256,2048]{1,0:T(8,128)}, f32[256,2048]{1,0:T(8,128)}, u32[]{:S(2)}, u32[]{:S(2)}) %collective-permute-start.39) | collective-permute-done | bytes 2097184 | tf_op jit(solution)/shard_map/ppermute | solution.py:210
  830.6 26.0 %collective-permute-done.32 = f32[384,1024]{1,0:T(8,128)S(1)} collective-permute-done((f32[384,1024]{1,0:T(8,128)S(1)}, f32[384,1024]{1,0:T(8,128)S(1)}, u32[]{:S(2)}, u32[]{:S(2)}) %collective-permute-start.32) | collective-permute-done | bytes 1572896 | tf_op jit(solution)/shard_map/ppermute | solution.py:210
  866.4 12.6 %collective-permute-done.13 = f32[128,2048]{1,0:T(8,128)S(1)} collective-permute-done((f32[128,2048]{1,0:T(8,128)}, f32[128,2048]{1,0:T(8,128)S(1)}, u32[]{:S(2)}, u32[]{:S(2)}) %collective-permute-start.13) | collective-permute-done | bytes 1048608 | tf_op jit(solution)/shard_map/ppermute | solution.py:210
  883.4 18.2 %collective-permute-done.37 = f32[128,2048]{1,0:T(8,128)} collective-permute-done((f32[128,2048]{1,0:T(8,128)}, f32[128,2048]{1,0:T(8,128)}, u32[]{:S(2)}, u32[]{:S(2)}) %collective-permute-start.37) | collective-permute-done | bytes 1048608 | tf_op jit(solution)/shard_map/ppermute | solution.py:210
  908.2 114.2 %collective-permute-done.14 = f32[64,2048]{1,0:T(8,128)S(1)} collective-permute-done((f32[64,2048]{1,0:T(8,128)S(1)}, f32[64,2048]{1,0:T(8,128)S(1)}, u32[]{:S(2)}, u32[]{:S(2)}) %collective-permute-start.14) | collective-permute-done | bytes 524320 | tf_op jit(solution)/shard_map/ppermute | solution.py:210
  1056.6 26.0 %collective-permute-done.28 = f32[128,3072]{1,0:T(8,128)S(1)} collective-permute-done((f32[128,3072]{1,0:T(8,128)S(1)}, f32[128,3072]{1,0:T(8,128)S(1)}, u32[]{:S(2)}, u32[]{:S(2)}) %collective-permute-start.28) | collective-permute-done | bytes 1572896 | tf_op jit(solution)/shard_map/ppermute | solution.py:210
  1086.7 29.7 %collective-permute-done.51 = f32[128,3072]{1,0:T(8,128)S(1)} collective-permute-done((f32[128,3072]{1,0:T(8,128)S(1)}, f32[128,3072]{1,0:T(8,128)S(1)}, u32[]{:S(2)}, u32[]{:S(2)}) %collective-permute-start.51) | collective-permute-done | bytes 1572896 | tf_op jit(solution)/shard_map/ppermute | solution.py:210
  1125.7 7.5 collective-permute-done.26
  (489 shorter events, 335.4 us)
Async XLA Ops:
  7.2 133.9 %all-gather.6.cloned.1.call-start = ((), (), s32[]{:S(2)}) async-start(), calls=%async_computation | async-start | bytes 33423360 | tf_op jit(solution)/shard_map/all_gather | solution.py:277
  13.6 219.9 %all-gather.8.cloned.1.call-start = ((), (), s32[]{:S(2)}) async-start(), calls=%async_computation.1 | async-start | bytes 22282240 | tf_op jit(solution)/shard_map/all_gather | solution.py:277
  19.9 290.3 %all-gather.10.cloned.1.call-start = ((), (), s32[]{:S(2)}) async-start(), calls=%async_computation.2 | async-start | bytes 11141120 | tf_op jit(solution)/shard_map/all_gather | solution.py:277
  177.0 126.1 %collective-permute-start.18 = (bf16[1024,384]{1,0:T(8,128)(2,1)}, bf16[1024,384]{1,0:T(8,128)(2,1)}, u32[]{:S(2)}, u32[]{:S(2)}) collective-permute-start(bf16[1024,384]{1,0:T(8,128)(2,1)} %get-tuple-element.69), channel_id=1, source_target_pairs={{0,1},{1,0},{2,3},{3,2},{4,5},{5,4},{6,7},{7,6},{8,9},{9,8},{10,11... | collective-permute-start | bytes 2359304 | tf_op jit(solution)/shard_map/ppermute | solution.py:169
  198.3 283.0 %collective-permute-start.30 = (bf16[1536,384]{1,0:T(8,128)(2,1)}, bf16[1536,384]{1,0:T(8,128)(2,1)}, u32[]{:S(2)}, u32[]{:S(2)}) collective-permute-start(bf16[1536,384]{1,0:T(8,128)(2,1)} %get-tuple-element.75), channel_id=1, source_target_pairs={{0,1},{1,0},{2,3},{3,2},{4,5},{5,4},{6,7},{7,6},{8,9},{9,8},{10,11... | collective-permute-start | bytes 3538952 | tf_op jit(solution)/shard_map/ppermute | solution.py:169
  221.8 74.1 %collective-permute-start.34 = (bf16[512,384]{1,0:T(8,128)(2,1)}, bf16[512,384]{1,0:T(8,128)(2,1)S(1)}, u32[]{:S(2)}, u32[]{:S(2)}) collective-permute-start(bf16[512,384]{1,0:T(8,128)(2,1)} %get-tuple-element.77), channel_id=1, source_target_pairs={{0,1},{1,0},{2,3},{3,2},{4,5},{5,4},{6,7},{7,6},{8,9},{9,8},{10,11... | collective-permute-start | bytes 1179656 | tf_op jit(solution)/shard_map/ppermute | solution.py:169
  301.4 191.6 %collective-permute-start.43 = (f32[512,1024]{1,0:T(8,128)}, f32[512,1024]{1,0:T(8,128)}, u32[]{:S(2)}, u32[]{:S(2)}) collective-permute-start(f32[512,1024]{1,0:T(8,128)} %fusion.140), channel_id=1, source_target_pairs={{0,8},{8,0},{1,9},{9,1},{2,10},{10,2},{3,11},{11,3},{4,12},{12,4},... | collective-permute-start | bytes 6291464 | tf_op jit(solution)/shard_map/ppermute | solution.py:210
  412.8 65.5 %collective-permute-start.19 = (bf16[384,1024]{1,0:T(8,128)(2,1)}, bf16[384,1024]{1,0:T(8,128)(2,1)}, u32[]{:S(2)}, u32[]{:S(2)}) collective-permute-start(bf16[384,1024]{1,0:T(8,128)(2,1)} %add_convert_fusion.1), channel_id=1, source_target_pairs={{0,1},{1,0},{2,3},{3,2},{4,5},{5,4},{6,7},{7,6},{8,9},{9,8},{10,11... | collective-permute-start | bytes 2359304 | tf_op jit(solution)/shard_map/ppermute | solution.py:169
  447.2 143.8 %collective-permute-start.11 = (bf16[384,4096]{1,0:T(8,128)(2,1)}, bf16[384,4096]{1,0:T(8,128)(2,1)}, u32[]{:S(2)}, u32[]{:S(2)}) collective-permute-start(bf16[384,4096]{1,0:T(8,128)(2,1)} %get-tuple-element.66), channel_id=1, source_target_pairs={{0,1},{1,0},{2,3},{3,2},{4,5},{5,4},{6,7},{7,6},{8,9},{9,8},{10,11... | collective-permute-start | bytes 9437192 | tf_op jit(solution)/shard_map/ppermute | solution.py:169
  486.8 101.4 %collective-permute-start.20 = (f32[512,1024]{1,0:T(8,128)S(1)}, f32[512,1024]{1,0:T(8,128)S(1)}, u32[]{:S(2)}, u32[]{:S(2)}) collective-permute-start(f32[512,1024]{1,0:T(8,128)S(1)} %fusion.142), channel_id=1, source_target_pairs={{0,8},{8,0},{1,9},{9,1},{2,10},{10,2},{3,11},{11,3},{4,12},{12,4},... | collective-permute-start | bytes 6291464 | tf_op jit(solution)/shard_map/ppermute | solution.py:210
  490.2 103.8 %collective-permute-start.53 = (f32[768,1024]{1,0:T(8,128)}, f32[768,1024]{1,0:T(8,128)S(1)}, u32[]{:S(2)}, u32[]{:S(2)}) collective-permute-start(f32[768,1024]{1,0:T(8,128)} %fusion.137), channel_id=1, source_target_pairs={{0,2},{2,0},{1,3},{3,1},{4,6},{6,4},{5,7},{7,5},{8,10},{10,8},{9,1... | collective-permute-start | bytes 9437192 | tf_op jit(solution)/shard_map/ppermute | solution.py:210
  491.5 68.3 %collective-permute-start.5 = (f32[512]{0:T(512)S(1)}, f32[512]{0:T(512)S(1)}, u32[]{:S(2)}, u32[]{:S(2)}) collective-permute-start(f32[512]{0:T(512)S(1)} %bitcast.170), channel_id=1, source_target_pairs={{0,6},{2,4},{4,2},{6,0},{8,14},{10,12},{12,10},{14,8},{1,7},{3,5},... | collective-permute-start | bytes 6152 | tf_op jit(solution)/shard_map/ppermute | solution.py:238
  493.1 66.7 %collective-permute-start.4 = (f32[512]{0:T(512)S(1)}, f32[512]{0:T(512)S(1)}, u32[]{:S(2)}, u32[]{:S(2)}) collective-permute-start(f32[512]{0:T(512)S(1)} %bitcast.169), channel_id=1, source_target_pairs={{0,4},{2,6},{4,0},{6,2},{8,12},{10,14},{12,8},{14,10},{1,5},{3,7},... | collective-permute-start | bytes 6152 | tf_op jit(solution)/shard_map/ppermute | solution.py:238
  585.4 150.5 %collective-permute-start.23 = (bf16[384,6144]{1,0:T(8,128)(2,1)S(1)}, bf16[384,6144]{1,0:T(8,128)(2,1)S(1)}, u32[]{:S(2)}, u32[]{:S(2)}) collective-permute-start(bf16[384,6144]{1,0:T(8,128)(2,1)S(1)} %bitcast.140), channel_id=1, source_target_pairs={{0,1},{1,0},{2,3},{3,2},{4,5},{5,4},{6,7},{7,6},{8,9},{9,8},{10,11... | collective-permute-start | bytes 14155784 | tf_op jit(solution)/shard_map/ppermute | solution.py:169
  588.1 151.6 %collective-permute-start.46 = (bf16[384,6144]{1,0:T(8,128)(2,1)S(1)}, bf16[384,6144]{1,0:T(8,128)(2,1)}, u32[]{:S(2)}, u32[]{:S(2)}) collective-permute-start(bf16[384,6144]{1,0:T(8,128)(2,1)S(1)} %bitcast.138), channel_id=1, source_target_pairs={{0,1},{1,0},{2,3},{3,2},{4,5},{5,4},{6,7},{7,6},{8,9},{9,8},{10,11... | collective-permute-start | bytes 14155784 | tf_op jit(solution)/shard_map/ppermute | solution.py:169
  591.0 99.3 %collective-permute-start.31 = (f32[768,1024]{1,0:T(8,128)}, f32[768,1024]{1,0:T(8,128)}, u32[]{:S(2)}, u32[]{:S(2)}) collective-permute-start(f32[768,1024]{1,0:T(8,128)} %fusion.135), channel_id=1, source_target_pairs={{0,2},{2,0},{1,3},{3,1},{4,6},{6,4},{5,7},{7,5},{8,10},{10,8},{9,1... | collective-permute-start | bytes 9437192 | tf_op jit(solution)/shard_map/ppermute | solution.py:210
  594.0 92.4 %collective-permute-start.45 = (f32[128,1024]{1,0:T(8,128)}, f32[128,1024]{1,0:T(8,128)}, u32[]{:S(2)}, u32[]{:S(2)}) collective-permute-start(f32[128,1024]{1,0:T(8,128)} %fusion.129), channel_id=1, source_target_pairs={{0,4},{4,0},{1,5},{5,1},{2,6},{6,2},{3,7},{7,3},{8,12},{12,8},{9,1... | collective-permute-start | bytes 1572872 | tf_op jit(solution)/shard_map/ppermute | solution.py:210
  598.2 86.0 %collective-permute-start.21 = (f32[256,1024]{1,0:T(8,128)}, f32[256,1024]{1,0:T(8,128)}, u32[]{:S(2)}, u32[]{:S(2)}) collective-permute-start(f32[256,1024]{1,0:T(8,128)} %convolution_add_fusion.25), channel_id=1, source_target_pairs={{0,2},{2,0},{1,3},{3,1},{4,6},{6,4},{5,7},{7,5},{8,10},{10,8},{9,1... | collective-permute-start | bytes 3145736 | tf_op jit(solution)/shard_map/ppermute | solution.py:210
  684.2 78.0 %collective-permute-start.54 = (f32[384,1024]{1,0:T(8,128)}, f32[384,1024]{1,0:T(8,128)}, u32[]{:S(2)}, u32[]{:S(2)}) collective-permute-start(f32[384,1024]{1,0:T(8,128)} %slice_add_fusion), channel_id=1, source_target_pairs={{0,4},{4,0},{1,5},{5,1},{2,6},{6,2},{3,7},{7,3},{8,12},{12,8},{9,1... | collective-permute-start | bytes 4718600 | tf_op jit(solution)/shard_map/ppermute | solution.py:210
  690.3 87.7 %collective-permute-start.15 = (f32[256,2048]{1,0:T(8,128)}, f32[256,2048]{1,0:T(8,128)}, u32[]{:S(2)}, u32[]{:S(2)}) collective-permute-start(f32[256,2048]{1,0:T(8,128)} %fusion.86), channel_id=1, source_target_pairs={{0,4},{4,0},{1,5},{5,1},{2,6},{6,2},{3,7},{7,3},{8,12},{12,8},{9,1... | collective-permute-start | bytes 6291464 | tf_op jit(solution)/shard_map/ppermute | solution.py:210
  738.2 84.7 %collective-permute-start.39 = (f32[256,2048]{1,0:T(8,128)}, f32[256,2048]{1,0:T(8,128)}, u32[]{:S(2)}, u32[]{:S(2)}) collective-permute-start(f32[256,2048]{1,0:T(8,128)} %fusion.76), channel_id=1, source_target_pairs={{0,4},{4,0},{1,5},{5,1},{2,6},{6,2},{3,7},{7,3},{8,12},{12,8},{9,1... | collective-permute-start | bytes 6291464 | tf_op jit(solution)/shard_map/ppermute | solution.py:210
  739.8 86.6 %collective-permute-start.36 = (f32[256,2048]{1,0:T(8,128)}, f32[256,2048]{1,0:T(8,128)}, u32[]{:S(2)}, u32[]{:S(2)}) collective-permute-start(f32[256,2048]{1,0:T(8,128)} %fusion.81), channel_id=1, source_target_pairs={{0,2},{2,0},{1,3},{3,1},{4,6},{6,4},{5,7},{7,5},{8,10},{10,8},{9,1... | collective-permute-start | bytes 6291464 | tf_op jit(solution)/shard_map/ppermute | solution.py:210
  762.2 94.3 %collective-permute-start.32 = (f32[384,1024]{1,0:T(8,128)S(1)}, f32[384,1024]{1,0:T(8,128)S(1)}, u32[]{:S(2)}, u32[]{:S(2)}) collective-permute-start(f32[384,1024]{1,0:T(8,128)S(1)} %copy-done.34), channel_id=1, source_target_pairs={{0,4},{4,0},{1,5},{5,1},{2,6},{6,2},{3,7},{7,3},{8,12},{12,8},{9,1... | collective-permute-start | bytes 4718600 | tf_op jit(solution)/shard_map/ppermute | solution.py:210
  778.0 81.8 %collective-permute-start.55 = (f32[192,1024]{1,0:T(8,128)}, f32[192,1024]{1,0:T(8,128)}, u32[]{:S(2)}, u32[]{:S(2)}) collective-permute-start(f32[192,1024]{1,0:T(8,128)} %fusion.128), channel_id=1, source_target_pairs={{0,8},{8,0},{1,9},{9,1},{2,10},{10,2},{3,11},{11,3},{4,12},{12,4},... | collective-permute-start | bytes 2359304 | tf_op jit(solution)/shard_map/ppermute | solution.py:210
  781.8 82.3 %collective-permute-start.16 = (f32[128,2048]{1,0:T(8,128)S(1)}, f32[128,2048]{1,0:T(8,128)S(1)}, u32[]{:S(2)}, u32[]{:S(2)}) collective-permute-start(f32[128,2048]{1,0:T(8,128)S(1)} %convolution_add_fusion.14), channel_id=1, source_target_pairs={{0,8},{8,0},{1,9},{9,1},{2,10},{10,2},{3,11},{11,3},{4,12},{12,4},... | collective-permute-start | bytes 3145736 | tf_op jit(solution)/shard_map/ppermute | solution.py:210
  864.0 180.5 %collective-permute-start.27 = (f32[256,3072]{1,0:T(8,128)}, f32[256,3072]{1,0:T(8,128)S(1)}, u32[]{:S(2)}, u32[]{:S(2)}) collective-permute-start(f32[256,3072]{1,0:T(8,128)} %fusion.49), channel_id=1, source_target_pairs={{0,8},{8,0},{1,9},{9,1},{2,10},{10,2},{3,11},{11,3},{4,12},{12,4},... | collective-permute-start | bytes 9437192 | tf_op jit(solution)/shard_map/ppermute | solution.py:210
  879.0 167.3 %collective-permute-start.24 = (f32[256,3072]{1,0:T(8,128)}, f32[256,3072]{1,0:T(8,128)S(1)}, u32[]{:S(2)}, u32[]{:S(2)}) collective-permute-start(f32[256,3072]{1,0:T(8,128)} %fusion.54), channel_id=1, source_target_pairs={{0,4},{4,0},{1,5},{5,1},{2,6},{6,2},{3,7},{7,3},{8,12},{12,8},{9,1... | collective-permute-start | bytes 9437192 | tf_op jit(solution)/shard_map/ppermute | solution.py:210
  881.3 167.0 %collective-permute-start.50 = (f32[256,3072]{1,0:T(8,128)}, f32[256,3072]{1,0:T(8,128)}, u32[]{:S(2)}, u32[]{:S(2)}) collective-permute-start(f32[256,3072]{1,0:T(8,128)} %fusion.39), channel_id=1, source_target_pairs={{0,8},{8,0},{1,9},{9,1},{2,10},{10,2},{3,11},{11,3},{4,12},{12,4},... | collective-permute-start | bytes 9437192 | tf_op jit(solution)/shard_map/ppermute | solution.py:210
  901.6 120.9 %collective-permute-start.14 = (f32[64,2048]{1,0:T(8,128)S(1)}, f32[64,2048]{1,0:T(8,128)S(1)}, u32[]{:S(2)}, u32[]{:S(2)}) collective-permute-start(f32[64,2048]{1,0:T(8,128)S(1)} %fusion.68), channel_id=1, source_target_pairs={{0,8},{8,0},{1,9},{9,1},{2,10},{10,2},{3,11},{11,3},{4,12},{12,4},... | collective-permute-start | bytes 1572872 | tf_op jit(solution)/shard_map/ppermute | solution.py:210
  907.7 144.4 %collective-permute-start.47 = (f32[256,3072]{1,0:T(8,128)}, f32[256,3072]{1,0:T(8,128)}, u32[]{:S(2)}, u32[]{:S(2)}) collective-permute-start(f32[256,3072]{1,0:T(8,128)} %fusion.44), channel_id=1, source_target_pairs={{0,4},{4,0},{1,5},{5,1},{2,6},{6,2},{3,7},{7,3},{8,12},{12,8},{9,1... | collective-permute-start | bytes 9437192 | tf_op jit(solution)/shard_map/ppermute | solution.py:210
  1050.6 65.8 %collective-permute-start.51 = (f32[128,3072]{1,0:T(8,128)S(1)}, f32[128,3072]{1,0:T(8,128)S(1)}, u32[]{:S(2)}, u32[]{:S(2)}) collective-permute-start(f32[128,3072]{1,0:T(8,128)S(1)} %convolution_add_fusion), channel_id=1, source_target_pairs={{0,2},{2,0},{1,3},{3,1},{4,6},{6,4},{5,7},{7,5},{8,10},{10,8},{9,1... | collective-permute-start | bytes 4718600 | tf_op jit(solution)/shard_map/ppermute | solution.py:210
  1054.3 65.7 %collective-permute-start.48 = (f32[128,3072]{1,0:T(8,128)S(1)}, f32[128,3072]{1,0:T(8,128)S(1)}, u32[]{:S(2)}, u32[]{:S(2)}) collective-permute-start(f32[128,3072]{1,0:T(8,128)S(1)} %convolution_add_fusion.1), channel_id=1, source_target_pairs={{0,8},{8,0},{1,9},{9,1},{2,10},{10,2},{3,11},{11,3},{4,12},{12,4},... | collective-permute-start | bytes 4718600 | tf_op jit(solution)/shard_map/ppermute | solution.py:210
  (133 other events, 1870.1 us)
Sparse Core Ops, SparseCore 0:
  13.7 127.3 all-gather.5
  143.3 90.0 all-gather.7
  236.3 55.9 all-gather.9
